TPU v7x, 32 devices: a whole 2x2x4 slice. The times are simulated.
32 devices in a mesh: dev: 32 (over z, y, x, core).
Axes of the slice: x: 2, y: 2, z: 4, core: 2. Of those that a mesh axis runs over, the one named last changes fastest.
Arguments:
- dual_blocks: bfloat16 [32, 3072, 3072], P('dev'), as said below
- rigid_modes: float32 [32, 6, 3072], P('dev'), may hold values from -5 to 5
- dual_local: float32 [32, 8, 3072], P('dev'), may hold values from -6 to 6
- coarse_rhs: float32 [32, 6, 8], P('dev'), may hold values from -4608 to 4608
- iface_sizes: int32 [32], P('dev'), may hold values from 1536 to 3072, as said below
- neighbours: int32 [32, 6], P('dev'), may hold values from -1 to 31, as said below
- shared_counts: int32 [32, 6], P('dev'), may hold values from 256 to 512, as said below
- iface_map: int32 [32, 3072], P('dev'), may hold values from -1 to 3071, as said below
- owner: int32 [32], replicated, may hold values from 0 to 31, as said below
Outputs:
- multipliers: float32 [32, 8, 3072], P('dev')
- projected_residual: float32 [32, 8, 3072], P('dev')
Inputs may be any that keep to these rules, and one draw needn't show every extreme that they name: `dual_blocks`: each block is symmetric positive definite, and so is each of its leading principal parts. Grid subdomain g is held by slot owner[g] = (g + s) mod 32 for one offset s of the draw, so the subdomains across the faces -x, +x, -y, +y, -z, +z of slot i sit in slots i - 1, i + 1, i - 4, i + 4, i - 16, i + 16, taken mod 32. `neighbours`: the subdomains form a grid of 4 x 4 x 32/16 with g = x + 4 y + 16 z. Row i lists, for the faces -x, +x, -y, +y, -z, +z of the subdomain held in slot i, the grid subdomain across that face, or -1 on the outer boundary; across a face from g the opposite face names g. `shared_counts`: equal on both sides of a shared face; some subdomain has 512 on all its faces. `iface_sizes`: the sum of the slot's shared_counts row; some subdomain has 3072. `iface_map`: for j < iface_sizes[i], entry j is f * 512 + p for the dof at position p of face f of slot i (p below that face's count), each such code once; -1 beyond. The dof at position p of a shared face pairs with the dof at position p of the opposite face of the neighbour.
All inputs are finite; a program needn't handle non-finite values.
Results may differ from a plain program's by a relative error of at most 0.025.
Values sent between devices are 32-bit elements; how exact they have to be, the bound alone decides.
A program may use at most 128 MiB of HBM per device.

v0:
```python
import jax
import jax.numpy as jnp
from jax import lax
from jax.sharding import PartitionSpec as P

FACES = 6
MODES = 6
CAP = 512
NMAX = 3072
ITERS = 3


HIGHEST_PRECISION = lax.Precision.HIGHEST
OPPOSITE = (1, 0, 3, 2, 5, 4)
FACE_STEPS = (-1, 1, -4, 4, -16, 16)


def from_behind(value, axis, by):
    length = lax.axis_size(axis)
    return lax.ppermute(value, axis, [(i, (i + by) % length) for i in range(length)])


def solve_coarse(factor, vector):
    middle = lax.linalg.triangular_solve(factor, vector, left_side=True, lower=True)
    return lax.linalg.triangular_solve(factor, middle, left_side=True, lower=True, transpose_a=True)


def per_device(
    dual_blocks,
    rigid_modes,
    dual_local,
    coarse_rhs,
    iface_sizes,
    neighbours,
    shared_counts,
    iface_map,
    owner,
):
    my_slot = lax.axis_index("dev")
    devices = lax.axis_size("dev")
    loads = dual_local.shape[1]
    columns = jnp.arange(NMAX, dtype=jnp.int32)
    live_dofs = columns < iface_sizes[0]
    dof_codes = jnp.clip(jnp.where(live_dofs, iface_map[0], 0), 0, FACES * CAP - 1)
    which_face = dof_codes // CAP
    position = dof_codes % CAP
    face_row = neighbours[0]
    count_row = shared_counts[0]
    face_onehot = which_face[None, :] == jnp.arange(FACES, dtype=jnp.int32)[:, None]
    has_partner = jnp.any(face_onehot & (face_row >= 0)[:, None], axis=0)
    face_limit = jnp.sum(jnp.where(face_onehot, count_row[:, None], 0), axis=0)
    shared = live_dofs & has_partner & (position < face_limit)
    live_float = live_dofs.astype(jnp.float32)
    shared_float = shared.astype(jnp.float32)
    weights = jnp.where(shared, 0.5, live_float)
    targets = jnp.where(live_dofs, dof_codes, FACES * CAP)
    inverse = (
        jnp.full((FACES * CAP,), NMAX, jnp.int32)
        .at[targets]
        .set(columns, mode="drop")
        .reshape(FACES, CAP)
    )
    partner_slot = jnp.where(face_row >= 0, owner[jnp.clip(face_row, 0, owner.shape[0] - 1)], 0)
    face_mask = (
        (face_row >= 0)[:, None] & (jnp.arange(CAP, dtype=jnp.int32)[None, :] < count_row[:, None])
    ).astype(jnp.float32)

    def gather_faces(values):
        padded = jnp.concatenate([values, jnp.zeros((values.shape[0], 1), values.dtype)], axis=1)
        return jnp.take(padded, inverse, axis=1)

    def across_faces(face_vals, mover):
        pieces = [mover(face_vals[:, OPPOSITE[face]], -FACE_STEPS[face]) for face in range(FACES)]
        return jnp.stack(pieces, axis=1) * face_mask[None]

    def spread_back(far_faces):
        flattened = far_faces.reshape(far_faces.shape[0], FACES * CAP)
        return jnp.take(flattened, dof_codes, axis=1) * shared_float[None]

    def combine(values, far_faces):
        return live_float[None] * (values - spread_back(far_faces))

    def partial_inner(left_vec, right_vec):
        return jnp.sum(weights[None] * left_vec * right_vec, axis=1)

    modes_live = rigid_modes[0] * live_float[None]
    local_rhs = dual_local[0]
    own_modes = gather_faces(modes_live)
    own_rhs = gather_faces(local_rhs)
    setup_pieces = [
        from_behind(
            (own_modes[:, OPPOSITE[face]], own_rhs[:, OPPOSITE[face]]), "dev", -FACE_STEPS[face]
        )
        for face in range(FACES)
    ]
    far_modes = jnp.stack([piece[0] for piece in setup_pieces], axis=1) * face_mask[None]
    far_rhs = jnp.stack([piece[1] for piece in setup_pieces], axis=1) * face_mask[None]
    dual_rhs = combine(local_rhs, far_rhs)
    diagonal = lax.dot_general(
        modes_live, modes_live, (((1,), (1,)), ((), ())), precision=HIGHEST_PRECISION
    )
    coupling = -jnp.einsum("afp,bfp->afb", own_modes, far_modes, precision=HIGHEST_PRECISION)
    block_row = jnp.zeros((MODES, devices, MODES), jnp.float32).at[:, my_slot, :].set(diagonal)
    block_row = block_row.at[:, partner_slot, :].add(coupling)
    coarse_matrix, coarse_goal = (
        lax.all_gather(block_row.reshape(MODES, devices * MODES), "dev", axis=0, tiled=True),
        lax.all_gather(coarse_rhs[0], "dev", axis=0, tiled=True),
    )
    factor = jnp.linalg.cholesky(coarse_matrix)

    def modes_apply(solution):
        stacked = solution.reshape(devices, MODES, loads)
        own_part = lax.dot_general(
            stacked[my_slot], modes_live, (((0,), (0,)), ((), ())), precision=HIGHEST_PRECISION
        )
        far_part = jnp.einsum(
            "bfp,fbl->lfp", far_modes, stacked[partner_slot], precision=HIGHEST_PRECISION
        )
        return combine(own_part, far_part)

    def project(residual):
        coarse_part = lax.dot_general(
            modes_live, residual, (((1,), (1,)), ((), ())), precision=HIGHEST_PRECISION
        )
        placed = jnp.zeros((devices, MODES, loads), jnp.float32).at[my_slot].set(coarse_part)
        coarse_all = lax.psum(placed, "dev").reshape(devices * MODES, loads)
        solution = solve_coarse(factor, coarse_all)
        projected = residual - modes_apply(solution)
        norm_sq = lax.psum(partial_inner(projected, projected), "dev")
        return (projected, norm_sq)

    def dual_apply(vector):
        products = lax.dot_general(
            vector.astype(jnp.bfloat16),
            dual_blocks[0],
            (((1,), (1,)), ((), ())),
            preferred_element_type=jnp.float32,
        )
        far_part = across_faces(
            gather_faces(products), lambda piece, offset: from_behind(piece, "dev", offset)
        )
        return combine(products, far_part)

    multipliers = modes_apply(solve_coarse(factor, coarse_goal))
    residual = dual_rhs - dual_apply(multipliers)
    projected, norm_sq = project(residual)
    direction = projected
    for step_index in range(ITERS):
        applied = dual_apply(direction)
        curvature = lax.psum(partial_inner(direction, applied), "dev")
        step_size = norm_sq / curvature
        multipliers = multipliers + step_size[:, None] * direction
        residual = residual - step_size[:, None] * applied
        projected, norm_next = project(residual)
        direction = projected + (norm_next / norm_sq)[:, None] * direction
        norm_sq = norm_next
    return (multipliers[None], projected[None])


def solution(mesh):
    return jax.shard_map(
        per_device,
        mesh=mesh,
        in_specs=(
            P("dev", None, None),
            P("dev", None, None),
            P("dev", None, None),
            P("dev", None, None),
            P("dev"),
            P("dev", None),
            P("dev", None),
            P("dev", None),
            P(),
        ),
        out_specs=(P("dev", None, None), P("dev", None, None)),
        check_vma=False,
    )
```

profile of v0, /device:TPU:0, one launch (start us, length us, event | category | flops | bytes accessed | tf_op | source)
XLA Modules:
  0.0 945.2 jit_solution(9198826558787820039)
XLA Ops:
  2.1 11.8 %scatter_custom_fusion = s32[3072]{0:T(1024)S(1)} fusion(s32[3072]{0:T(1024)S(1)} %bitcast.527, s32[3072]{0:T(1024)S(1)} %iota.115, s32[]{:T(128)} %constant.261.clone.1), kind=kCustom, calls=%fused_computation.314 | custom fusion | bytes 12292 | tf_op jit(solution)/shard_map/scatter | solution.py:60
  16.0 10.9 %gather_fusion.1 = f32[3072,6]{1,0:T(8,128)} fusion(f32[6,3073]{0,1:T(8,128)S(1)} %concatenate.51, s32[3072]{0:T(1024)S(1)} %broadcast_clamp_fusion.1), kind=kCustom, calls=%fused_computation.16 | custom fusion | bytes 159744 | tf_op jit(solution)/shard_map/jit(_take)/gather | solution.py:70
  30.0 5.9 collective-permute-start.1
  36.0 4.7 collective-permute-start.3
  47.6 36.6 %all-gather = f32[1,192,8]{2,0,1:T(1,128)S(1)} all-gather(f32[1,6,8]{2,0,1:T(1,128)S(1)} %copy-done.67), channel_id=2, replica_groups=mesh['dev'=32] {'dev'}, dimensions={1}, use_global_device_ids=true | all-gather | bytes 6336 | tf_op jit(solution)/shard_map/all_gather | solution.py:107
  86.1 9.5 %gather_fusion.8 = f32[3072,8]{1,0:T(8,128)S(1)} fusion(f32[8,3073]{0,1:T(8,128)} %concatenate.52.clone, s32[3072]{0:T(1024)S(1)} %get-tuple-element.217), kind=kCustom, calls=%fused_computation.1.clone | custom fusion | bytes 208896 | tf_op jit(solution)/shard_map/jit(_take)/gather | solution.py:70
  104.8 39.5 %all-gather.1 = f32[32,6,192]{2,1,0:T(8,128)S(1)} all-gather(f32[1,6,192]{2,1,0:T(8,128)S(1)} %reshape.887), channel_id=1, replica_groups=mesh['dev'=32] {'dev'}, dimensions={0}, use_global_device_ids=true | all-gather | bytes 152064 | tf_op jit(solution)/shard_map/all_gather | solution.py:106
  144.5 11.7 %cholesky.51 = f32[128,128]{1,0:T(8,128)S(1)} custom-call(f32[128,128]{1,0:T(8,128)S(1)} %cholesky.124), custom_call_target="Cholesky" | custom-call | tf_op jit(solution)/shard_map/jit(cholesky)/cholesky | solution.py:109
  156.2 9.8 %custom-call.17 = f32[1,128,128]{1,2,0:T(8,128)S(1)} custom-call(f32[1,128,128]{2,1,0:T(8,128)S(1)} %get-tuple-element.201), custom_call_target="InvertDiagBlocksLowerTriangular" | custom-call | tf_op jit(solution)/shard_map/jit(cholesky)/cholesky | solution.py:109
  166.4 5.8 cholesky.110
  175.0 19.8 %custom-call.27 = f32[2,128,128]{1,2,0:T(8,128)S(1)} custom-call(f32[2,128,128]{2,1,0:T(8,128)S(1)} %pad_maximum_fusion), custom_call_target="InvertDiagBlocksLowerTriangular" | custom-call | tf_op jit(solution)/shard_map/triangular_solve/custom-call.4 | solution.py:25
  199.3 10.9 %gather_fusion.7 = f32[3072,8]{1,0:T(8,128)} fusion(f32[8,3072]{0,1:T(8,128)S(1)} %copy.143, s32[3072]{0:T(1024)S(1)} %get-tuple-element.216), kind=kCustom, calls=%fused_computation.clone | custom fusion | bytes 208896 | tf_op jit(solution)/shard_map/jit(_take)/gather | solution.py:78
  212.9 12.0 %fusion.6 = f32[8,3072]{1,0:T(8,128)} fusion(bf16[1,3072,3072]{2,1,0:T(8,128)(2,1)} %param.27, f32[8,3072]{1,0:T(8,128)S(1)} %fusion.17), kind=kOutput, calls=%fused_computation.30 | convolution fusion | flops 151019520 | bytes 19070976 | tf_op jit(solution)/shard_map/dot_general | solution.py:133
  227.6 9.5 %gather_fusion.10 = f32[3072,8]{1,0:T(8,128)S(1)} fusion(f32[8,3073]{0,1:T(8,128)} %concatenate.53.clone, s32[3072]{0:T(1024)S(1)} %get-tuple-element.217), kind=kCustom, calls=%fused_computation.11.clone | custom fusion | bytes 208896 | tf_op jit(solution)/shard_map/jit(_take)/gather | solution.py:70
  239.6 5.0 collective-permute-start.7
  244.6 4.7 collective-permute-start.9
  249.4 6.7 collective-permute-done.12
  258.0 4.7 collective-permute-start.15
  277.0 12.6 %gather_fusion.11 = f32[3072,8]{1,0:T(8,128)} fusion(f32[8,3072]{0,1:T(8,128)} %get-tuple-element.205, s32[3072]{0:T(1024)S(1)} %get-tuple-element.216), kind=kCustom, calls=%fused_computation.3.clone | custom fusion | bytes 208896 | tf_op jit(solution)/shard_map/jit(_take)/gather | solution.py:78
  292.1 10.9 %gather_fusion.9 = f32[3072,8]{1,0:T(8,128)} fusion(f32[8,3072]{0,1:T(8,128)S(1)} %copy-done.2, s32[3072]{0:T(1024)S(1)} %get-tuple-element.216), kind=kCustom, calls=%fused_computation.2.clone | custom fusion | bytes 208896 | tf_op jit(solution)/shard_map/jit(_take)/gather | solution.py:78
  309.2 37.8 %psum.70 = f32[192,8]{0,1:T(8,128)S(1)} all-reduce(f32[192,8]{0,1:T(8,128)S(1)} %reshape.519), channel_id=1, replica_groups=mesh['dev'=32] {'dev'}, use_global_device_ids=true, to_apply=%region_10.15 | all-reduce | flops 1536 | bytes 12288 | tf_op jit(solution)/shard_map/psum | solution.py:126
  353.6 10.9 %gather_fusion.12 = f32[3072,8]{1,0:T(8,128)} fusion(f32[8,3072]{0,1:T(8,128)S(1)} %copy.157, s32[3072]{0:T(1024)S(1)} %get-tuple-element.216), kind=kCustom, calls=%fused_computation.4.clone | custom fusion | bytes 208896 | tf_op jit(solution)/shard_map/jit(_take)/gather | solution.py:78
  366.6 12.0 %fusion.4 = f32[8,3072]{1,0:T(8,128)} fusion(bf16[1,3072,3072]{2,1,0:T(8,128)(2,1)} %param.27, f32[8,3072]{1,0:T(8,128)S(1)} %fusion.16), kind=kOutput, calls=%fused_computation.28 | convolution fusion | flops 151019520 | bytes 19070976 | tf_op jit(solution)/shard_map/dot_general | solution.py:133
  381.3 11.0 %gather_fusion.13 = f32[3072,8]{1,0:T(8,128)S(1)} fusion(f32[8,3073]{0,1:T(8,128)} %concatenate.55.clone, s32[3072]{0:T(1024)} %copy-done.45), kind=kCustom, calls=%fused_computation.12.clone | custom fusion | bytes 208896 | tf_op jit(solution)/shard_map/jit(_take)/gather | solution.py:70
  394.4 5.3 collective-permute-start.19
  399.7 4.7 collective-permute-start.21
  414.7 13.8 %gather_fusion.14 = f32[3072,8]{1,0:T(8,128)} fusion(f32[8,3072]{0,1:T(8,128)} %bitcast_multiply_fusion.2, s32[3072]{0:T(1024)} %copy-done.34), kind=kCustom, calls=%fused_computation.5.clone | custom fusion | bytes 208896 | tf_op jit(solution)/shard_map/jit(_take)/gather | solution.py:78
  430.6 38.5 %all-reduce.11 = (f32[8]{0:T(128)S(1)}, f32[8]{0:T(128)S(1)}) all-reduce(f32[8]{0:T(128)S(1)} %get-tuple-element.155, f32[8]{0:T(128)S(1)} %get-tuple-element.154), channel_id=1, replica_groups=mesh['dev'=32] {'dev'}, use_global_device_ids=true, to_apply=%region_12.17 | all-reduce | flops 16 | bytes 128 | tf_op jit(solution)/shard_map/psum | solution.py:129
  473.3 39.3 %psum.73 = f32[192,8]{0,1:T(8,128)S(1)} all-reduce(f32[192,8]{0,1:T(8,128)S(1)} %reshape.523), channel_id=1, replica_groups=mesh['dev'=32] {'dev'}, use_global_device_ids=true, to_apply=%region_15.20 | all-reduce | flops 1536 | bytes 12288 | tf_op jit(solution)/shard_map/psum | solution.py:126
  518.6 10.9 %gather_fusion.15 = f32[3072,8]{1,0:T(8,128)} fusion(f32[8,3072]{0,1:T(8,128)S(1)} %copy.167, s32[3072]{0:T(1024)S(1)} %copy-done.35), kind=kCustom, calls=%fused_computation.6.clone | custom fusion | bytes 208896 | tf_op jit(solution)/shard_map/jit(_take)/gather | solution.py:78
  531.8 40.7 %psum.74 = f32[8]{0:T(128)S(1)} all-reduce(f32[8]{0:T(128)S(1)} %get-tuple-element.210), channel_id=1, replica_groups=mesh['dev'=32] {'dev'}, use_global_device_ids=true, to_apply=%region_17.22 | all-reduce | flops 8 | bytes 64 | tf_op jit(solution)/shard_map/psum | solution.py:129
  573.2 12.0 %fusion.2 = f32[8,3072]{1,0:T(8,128)} fusion(bf16[1,3072,3072]{2,1,0:T(8,128)(2,1)} %param.27, f32[8,3072]{1,0:T(8,128)S(1)} %multiply_add_fusion.1), kind=kOutput, calls=%fused_computation.26 | convolution fusion | flops 151019520 | bytes 19070976 | tf_op jit(solution)/shard_map/dot_general | solution.py:133
  587.9 11.0 %gather_fusion.16 = f32[3072,8]{1,0:T(8,128)S(1)} fusion(f32[8,3073]{0,1:T(8,128)} %concatenate.56.clone, s32[3072]{0:T(1024)} %copy-done.45), kind=kCustom, calls=%fused_computation.13.clone | custom fusion | bytes 208896 | tf_op jit(solution)/shard_map/jit(_take)/gather | solution.py:70
  600.9 5.3 collective-permute-start.25
  606.2 4.9 collective-permute-start.27
  621.4 13.4 %gather_fusion.17 = f32[3072,8]{1,0:T(8,128)} fusion(f32[8,3072]{0,1:T(8,128)} %bitcast_multiply_fusion.1, s32[3072]{0:T(1024)} %copy-done.34), kind=kCustom, calls=%fused_computation.7.clone | custom fusion | bytes 208896 | tf_op jit(solution)/shard_map/jit(_take)/gather | solution.py:78
  636.9 38.5 %psum.75 = f32[8]{0:T(128)S(1)} all-reduce(f32[8]{0:T(128)S(1)} %multiply_reduce_fusion.1), channel_id=1, replica_groups=mesh['dev'=32] {'dev'}, use_global_device_ids=true, to_apply=%region_19.24 | all-reduce | flops 8 | bytes 64 | tf_op jit(solution)/shard_map/psum | solution.py:150
  679.7 39.3 %psum.76 = f32[192,8]{0,1:T(8,128)S(1)} all-reduce(f32[192,8]{0,1:T(8,128)S(1)} %reshape.527), channel_id=1, replica_groups=mesh['dev'=32] {'dev'}, use_global_device_ids=true, to_apply=%region_20.25 | all-reduce | flops 1536 | bytes 12288 | tf_op jit(solution)/shard_map/psum | solution.py:126
  725.5 11.9 %gather_fusion.18 = f32[3072,8]{1,0:T(8,128)} fusion(f32[8,3072]{0,1:T(8,128)S(1)} %copy.177, s32[3072]{0:T(1024)} %copy-done.34), kind=kCustom, calls=%fused_computation.8.clone | custom fusion | bytes 208896 | tf_op jit(solution)/shard_map/jit(_take)/gather | solution.py:78
  739.8 40.8 %psum.77 = f32[8]{0:T(128)S(1)} all-reduce(f32[8]{0:T(128)S(1)} %get-tuple-element.212), channel_id=1, replica_groups=mesh['dev'=32] {'dev'}, use_global_device_ids=true, to_apply=%region_22.27 | all-reduce | flops 8 | bytes 64 | tf_op jit(solution)/shard_map/psum | solution.py:129
  781.1 12.0 %fusion = f32[8,3072]{1,0:T(8,128)} fusion(bf16[1,3072,3072]{2,1,0:T(8,128)(2,1)} %param.27, f32[8,3072]{1,0:T(8,128)S(1)} %get-tuple-element.213, f32[8,3072]{1,0:T(8,128)S(1)} %multiply_add_fusion.1, f32[8]{0:T(128)S(1)} %div.44), kind=kOutput, calls=%fused_computation.24 | convolution fusion | flops 151068672 | bytes 19169312 | tf_op jit(solution)/shard_map/dot_general | solution.py:133
  795.8 11.0 %gather_fusion.19 = f32[3072,8]{1,0:T(8,128)S(1)} fusion(f32[8,3073]{0,1:T(8,128)} %concatenate.57.clone, s32[3072]{0:T(1024)} %copy-done.45), kind=kCustom, calls=%fused_computation.14.clone | custom fusion | bytes 208896 | tf_op jit(solution)/shard_map/jit(_take)/gather | solution.py:70
  808.8 5.3 collective-permute-start.31
  814.2 4.7 collective-permute-start.33
  829.2 13.5 %gather_fusion.20 = f32[3072,8]{1,0:T(8,128)} fusion(f32[8,3072]{0,1:T(8,128)} %bitcast_multiply_fusion, s32[3072]{0:T(1024)} %copy-done.34), kind=kCustom, calls=%fused_computation.9.clone | custom fusion | bytes 208896 | tf_op jit(solution)/shard_map/jit(_take)/gather | solution.py:78
  844.8 38.5 %psum.78 = f32[8]{0:T(128)S(1)} all-reduce(f32[8]{0:T(128)S(1)} %get-tuple-element.158), channel_id=1, replica_groups=mesh['dev'=32] {'dev'}, use_global_device_ids=true, to_apply=%region_24.29 | all-reduce | flops 8 | bytes 64 | tf_op jit(solution)/shard_map/psum | solution.py:150
  887.7 39.3 %psum.79 = f32[192,8]{0,1:T(8,128)S(1)} all-reduce(f32[192,8]{0,1:T(8,128)S(1)} %reshape.531), channel_id=1, replica_groups=mesh['dev'=32] {'dev'}, use_global_device_ids=true, to_apply=%region_25.30 | all-reduce | flops 1536 | bytes 12288 | tf_op jit(solution)/shard_map/psum | solution.py:126
  931.5 10.9 %gather_fusion.21 = f32[3072,8]{1,0:T(8,128)} fusion(f32[8,3072]{0,1:T(8,128)S(1)} %copy.187, s32[3072]{0:T(1024)S(1)} %copy-done.36), kind=kCustom, calls=%fused_computation.10.clone | custom fusion | bytes 208896 | tf_op jit(solution)/shard_map/jit(_take)/gather | solution.py:78
  (471 shorter events, 160.6 us)
Async XLA Ops:
  15.4 289.5 %copy-start.9 = (f32[3072]{0:T(1024)}, f32[3072]{0:T(1024)S(1)}, u32[]{:S(2)}) copy-start(f32[3072]{0:T(1024)S(1)} %get-tuple-element.214) | copy-start | bytes 36868
  26.9 57.4 %copy-start.51 = (f32[1,8,3072]{2,1,0:T(8,128)S(1)}, f32[1,8,3072]{2,1,0:T(8,128)}, u32[]{:S(2)}) copy-start(f32[1,8,3072]{2,1,0:T(8,128)} %param.29) | copy-start | bytes 294916
  28.9 55.9 %copy-start.58 = (pred[6,512]{1,0:T(8,128)(4,1)}, pred[6,512]{1,0:T(8,128)(4,1)S(1)}, u32[]{:S(2)}) copy-start(pred[6,512]{1,0:T(8,128)(4,1)S(1)} %compare_and_fusion.1) | copy-start | bytes 9220
  29.5 67.2 %collective-permute-start = (f32[6,512]{1,0:T(8,128)}, f32[6,512]{1,0:T(8,128)}, u32[]{:S(2)}, u32[]{:S(2)}) collective-permute-start(f32[6,512]{1,0:T(8,128)} %get-tuple-element.199), channel_id=1, source_target_pairs={{0,1},{1,2},{2,3},{3,4},{4,5},{5,6},{6,7},{7,8},{8,9},{9,10},{10,1... | collective-permute-start | bytes 36872 | tf_op jit(solution)/shard_map/ppermute | solution.py:20
  30.0 67.4 %collective-permute-start.1 = (f32[6,512]{1,0:T(8,128)}, f32[6,512]{1,0:T(8,128)}, u32[]{:S(2)}, u32[]{:S(2)}) collective-permute-start(f32[6,512]{1,0:T(8,128)} %get-tuple-element.198), channel_id=1, source_target_pairs={{0,31},{1,0},{2,1},{3,2},{4,3},{5,4},{6,5},{7,6},{8,7},{9,8},{10,9... | collective-permute-start | bytes 36872 | tf_op jit(solution)/shard_map/ppermute | solution.py:20
  36.0 62.2 %collective-permute-start.2 = (f32[6,512]{1,0:T(8,128)}, f32[6,512]{1,0:T(8,128)}, u32[]{:S(2)}, u32[]{:S(2)}) collective-permute-start(f32[6,512]{1,0:T(8,128)} %get-tuple-element.197), channel_id=1, source_target_pairs={{0,4},{1,5},{2,6},{3,7},{4,8},{5,9},{6,10},{7,11},{8,12},{9,13},{1... | collective-permute-start | bytes 36872 | tf_op jit(solution)/shard_map/ppermute | solution.py:20
  36.0 62.9 %collective-permute-start.3 = (f32[6,512]{1,0:T(8,128)}, f32[6,512]{1,0:T(8,128)}, u32[]{:S(2)}, u32[]{:S(2)}) collective-permute-start(f32[6,512]{1,0:T(8,128)} %get-tuple-element.196), channel_id=1, source_target_pairs={{0,28},{1,29},{2,30},{3,31},{4,0},{5,1},{6,2},{7,3},{8,4},{9,5},{1... | collective-permute-start | bytes 36872 | tf_op jit(solution)/shard_map/ppermute | solution.py:20
  40.7 58.9 %collective-permute-start.4 = (f32[6,512]{1,0:T(8,128)}, f32[6,512]{1,0:T(8,128)}, u32[]{:S(2)}, u32[]{:S(2)}) collective-permute-start(f32[6,512]{1,0:T(8,128)} %get-tuple-element.195), channel_id=1, source_target_pairs={{0,16},{1,17},{2,18},{3,19},{4,20},{5,21},{6,22},{7,23},{8,24},{9,... | collective-permute-start | bytes 36872 | tf_op jit(solution)/shard_map/ppermute | solution.py:20
  41.2 310.1 %copy-start.41 = (f32[6,512]{1,0:T(8,128)}, f32[6,512]{1,0:T(8,128)S(1)}, u32[]{:S(2)}) copy-start(f32[6,512]{1,0:T(8,128)S(1)} %fusion.91) | copy-start | bytes 36868
  44.1 183.5 %copy-start.45 = (s32[3072]{0:T(1024)}, s32[3072]{0:T(1024)S(1)}, u32[]{:S(2)}) copy-start(s32[3072]{0:T(1024)S(1)} %get-tuple-element.217) | copy-start | bytes 36868
  44.1 309.5 %copy-start.34 = (s32[3072]{0:T(1024)}, s32[3072]{0:T(1024)S(1)}, u32[]{:S(2)}) copy-start(s32[3072]{0:T(1024)S(1)} %get-tuple-element.216) | copy-start | bytes 36868
  46.3 226.9 %copy-start.54 = (f32[3072]{0:T(1024)}, f32[3072]{0:T(1024)S(1)}, u32[]{:S(2)}) copy-start(f32[3072]{0:T(1024)S(1)} %and_convert_fusion) | copy-start | bytes 36868
  84.3 220.6 %copy-start.17 = (f32[1,3072]{1,0:T(1,128)}, f32[1,3072]{1,0:T(1,128)S(1)}, u32[]{:S(2)}) copy-start(f32[1,3072]{1,0:T(1,128)S(1)} %mul.372) | copy-start | bytes 36868
  96.7 4.6 collective-permute-start.5
  104.8 70.1 %copy-start.56 = (f32[128,64]{1,0:T(8,128)S(1)}, f32[128,64]{1,0:T(8,128)}, u32[]{:S(2)}) copy-start(f32[128,64]{1,0:T(8,128)} %pad_convert_fusion) | copy-start | bytes 98308
  239.2 10.1 %collective-permute-start.6 = (f32[8,512]{1,0:T(8,128)S(1)}, f32[8,512]{1,0:T(8,128)S(1)}, u32[]{:S(2)}, u32[]{:S(2)}) collective-permute-start(f32[8,512]{1,0:T(8,128)S(1)} %get-tuple-element.187), channel_id=1, source_target_pairs={{0,1},{1,2},{2,3},{3,4},{4,5},{5,6},{6,7},{7,8},{8,9},{9,10},{10,1... | collective-permute-start | bytes 49160 | tf_op jit(solution)/shard_map/ppermute | solution.py:20
  239.6 18.3 %collective-permute-start.7 = (f32[8,512]{1,0:T(8,128)S(1)}, f32[8,512]{1,0:T(8,128)S(1)}, u32[]{:S(2)}, u32[]{:S(2)}) collective-permute-start(f32[8,512]{1,0:T(8,128)S(1)} %get-tuple-element.186), channel_id=1, source_target_pairs={{0,31},{1,0},{2,1},{3,2},{4,3},{5,4},{6,5},{7,6},{8,7},{9,8},{10,9... | collective-permute-start | bytes 49160 | tf_op jit(solution)/shard_map/ppermute | solution.py:20
  244.6 13.4 %collective-permute-start.8 = (f32[8,512]{1,0:T(8,128)S(1)}, f32[8,512]{1,0:T(8,128)S(1)}, u32[]{:S(2)}, u32[]{:S(2)}) collective-permute-start(f32[8,512]{1,0:T(8,128)S(1)} %get-tuple-element.185), channel_id=1, source_target_pairs={{0,4},{1,5},{2,6},{3,7},{4,8},{5,9},{6,10},{7,11},{8,12},{9,13},{1... | collective-permute-start | bytes 49160 | tf_op jit(solution)/shard_map/ppermute | solution.py:20
  244.6 13.4 %collective-permute-start.9 = (f32[8,512]{1,0:T(8,128)S(1)}, f32[8,512]{1,0:T(8,128)S(1)}, u32[]{:S(2)}, u32[]{:S(2)}) collective-permute-start(f32[8,512]{1,0:T(8,128)S(1)} %get-tuple-element.184), channel_id=1, source_target_pairs={{0,28},{1,29},{2,30},{3,31},{4,0},{5,1},{6,2},{7,3},{8,4},{9,5},{1... | collective-permute-start | bytes 49160 | tf_op jit(solution)/shard_map/ppermute | solution.py:20
  249.3 13.4 %collective-permute-start.10 = (f32[8,512]{1,0:T(8,128)S(1)}, f32[8,512]{1,0:T(8,128)S(1)}, u32[]{:S(2)}, u32[]{:S(2)}) collective-permute-start(f32[8,512]{1,0:T(8,128)S(1)} %get-tuple-element.183), channel_id=1, source_target_pairs={{0,16},{1,17},{2,18},{3,19},{4,20},{5,21},{6,22},{7,23},{8,24},{9,... | collective-permute-start | bytes 49160 | tf_op jit(solution)/shard_map/ppermute | solution.py:20
  249.3 6.8 collective-permute-start.12
  256.1 6.6 collective-permute-start.11
  257.9 7.8 collective-permute-start.13
  257.9 8.3 collective-permute-start.14
  258.0 8.9 collective-permute-start.15
  262.7 4.8 collective-permute-start.16
  262.7 6.7 collective-permute-start.17
  366.6 63.8 %copy-start.3 = (f32[8,3072]{1,0:T(8,128)}, f32[8,3072]{1,0:T(8,128)S(1)}, u32[]{:S(2)}) copy-start(f32[8,3072]{1,0:T(8,128)S(1)} %fusion.16) | copy-start | bytes 294916
  394.3 10.1 %collective-permute-start.18 = (f32[8,512]{1,0:T(8,128)S(1)}, f32[8,512]{1,0:T(8,128)S(1)}, u32[]{:S(2)}, u32[]{:S(2)}) collective-permute-start(f32[8,512]{1,0:T(8,128)S(1)} %get-tuple-element.181), channel_id=1, source_target_pairs={{0,1},{1,2},{2,3},{3,4},{4,5},{5,6},{6,7},{7,8},{8,9},{9,10},{10,1... | collective-permute-start | bytes 49160 | tf_op jit(solution)/shard_map/ppermute | solution.py:20
  394.4 13.6 %collective-permute-start.19 = (f32[8,512]{1,0:T(8,128)S(1)}, f32[8,512]{1,0:T(8,128)S(1)}, u32[]{:S(2)}, u32[]{:S(2)}) collective-permute-start(f32[8,512]{1,0:T(8,128)S(1)} %get-tuple-element.180), channel_id=1, source_target_pairs={{0,31},{1,0},{2,1},{3,2},{4,3},{5,4},{6,5},{7,6},{8,7},{9,8},{10,9... | collective-permute-start | bytes 49160 | tf_op jit(solution)/shard_map/ppermute | solution.py:20
  399.7 8.9 collective-permute-start.20
  399.7 9.5 %collective-permute-start.21 = (f32[8,512]{1,0:T(8,128)S(1)}, f32[8,512]{1,0:T(8,128)S(1)}, u32[]{:S(2)}, u32[]{:S(2)}) collective-permute-start(f32[8,512]{1,0:T(8,128)S(1)} %get-tuple-element.178), channel_id=1, source_target_pairs={{0,28},{1,29},{2,30},{3,31},{4,0},{5,1},{6,2},{7,3},{8,4},{9,5},{1... | collective-permute-start | bytes 49160 | tf_op jit(solution)/shard_map/ppermute | solution.py:20
  404.4 5.3 collective-permute-start.22
  404.4 5.9 collective-permute-start.23
  414.7 55.0 %copy-start.33 = (f32[8,3072]{1,0:T(8,128)S(1)}, f32[8,3072]{1,0:T(8,128)}, u32[]{:S(2)}) copy-start(f32[8,3072]{1,0:T(8,128)} %copy-done.31) | copy-start | bytes 294916
  600.8 10.3 %collective-permute-start.24 = (f32[8,512]{1,0:T(8,128)S(1)}, f32[8,512]{1,0:T(8,128)S(1)}, u32[]{:S(2)}, u32[]{:S(2)}) collective-permute-start(f32[8,512]{1,0:T(8,128)S(1)} %get-tuple-element.175), channel_id=1, source_target_pairs={{0,1},{1,2},{2,3},{3,4},{4,5},{5,6},{6,7},{7,8},{8,9},{9,10},{10,1... | collective-permute-start | bytes 49160 | tf_op jit(solution)/shard_map/ppermute | solution.py:20
  600.9 13.7 %collective-permute-start.25 = (f32[8,512]{1,0:T(8,128)S(1)}, f32[8,512]{1,0:T(8,128)S(1)}, u32[]{:S(2)}, u32[]{:S(2)}) collective-permute-start(f32[8,512]{1,0:T(8,128)S(1)} %get-tuple-element.174), channel_id=1, source_target_pairs={{0,31},{1,0},{2,1},{3,2},{4,3},{5,4},{6,5},{7,6},{8,7},{9,8},{10,9... | collective-permute-start | bytes 49160 | tf_op jit(solution)/shard_map/ppermute | solution.py:20
  606.2 9.0 collective-permute-start.26
  606.2 9.6 %collective-permute-start.27 = (f32[8,512]{1,0:T(8,128)S(1)}, f32[8,512]{1,0:T(8,128)S(1)}, u32[]{:S(2)}, u32[]{:S(2)}) collective-permute-start(f32[8,512]{1,0:T(8,128)S(1)} %get-tuple-element.172), channel_id=1, source_target_pairs={{0,28},{1,29},{2,30},{3,31},{4,0},{5,1},{6,2},{7,3},{8,4},{9,5},{1... | collective-permute-start | bytes 49160 | tf_op jit(solution)/shard_map/ppermute | solution.py:20
  611.1 5.3 collective-permute-start.28
  611.1 5.9 collective-permute-start.29
  808.8 10.1 %collective-permute-start.30 = (f32[8,512]{1,0:T(8,128)S(1)}, f32[8,512]{1,0:T(8,128)S(1)}, u32[]{:S(2)}, u32[]{:S(2)}) collective-permute-start(f32[8,512]{1,0:T(8,128)S(1)} %get-tuple-element.169), channel_id=1, source_target_pairs={{0,1},{1,2},{2,3},{3,4},{4,5},{5,6},{6,7},{7,8},{8,9},{9,10},{10,1... | collective-permute-start | bytes 49160 | tf_op jit(solution)/shard_map/ppermute | solution.py:20
  808.8 13.6 %collective-permute-start.31 = (f32[8,512]{1,0:T(8,128)S(1)}, f32[8,512]{1,0:T(8,128)S(1)}, u32[]{:S(2)}, u32[]{:S(2)}) collective-permute-start(f32[8,512]{1,0:T(8,128)S(1)} %get-tuple-element.168), channel_id=1, source_target_pairs={{0,31},{1,0},{2,1},{3,2},{4,3},{5,4},{6,5},{7,6},{8,7},{9,8},{10,9... | collective-permute-start | bytes 49160 | tf_op jit(solution)/shard_map/ppermute | solution.py:20
  814.1 8.9 collective-permute-start.32
  814.2 9.5 %collective-permute-start.33 = (f32[8,512]{1,0:T(8,128)S(1)}, f32[8,512]{1,0:T(8,128)S(1)}, u32[]{:S(2)}, u32[]{:S(2)}) collective-permute-start(f32[8,512]{1,0:T(8,128)S(1)} %get-tuple-element.166), channel_id=1, source_target_pairs={{0,28},{1,29},{2,30},{3,31},{4,0},{5,1},{6,2},{7,3},{8,4},{9,5},{1... | collective-permute-start | bytes 49160 | tf_op jit(solution)/shard_map/ppermute | solution.py:20
  818.9 5.3 collective-permute-start.34
  818.9 5.9 collective-permute-start.35
  829.2 54.2 %copy-start.81 = (f32[8]{0:T(128)S(1)}, f32[8]{0:T(128)}, u32[]{:S(2)}) copy-start(f32[8]{0:T(128)} %copy-done.80) | copy-start | bytes 100
  (70 other events, 1357.1 us)
where the time goes:
time: 954 us; the launch traced here: 945 us
  blocking collectives  429 us (45%)
  local copies, waits for them, and re-layouts  283 us (30%)
  matrix products  80.1 us (8%)
  other arithmetic  72 us (8%)
  starting transfers between devices  69.4 us (7%)
    psum x4, blocking collectives, project(): coarse_all = lax.psum(placed, 'dev').reshape(devices * MODES, loads)  156 us
    gather x20, local copies, waits for them, and re-layouts, spread_back(): return jnp.take(flattened, dof_codes, axis=1) * shared_float[None]  139 us
    psum x3, blocking collectives, project(): norm_sq = lax.psum(partial_inner(projected, projected), 'dev')  120 us
    psum x2, blocking collectives, per_device(): curvature = lax.psum(partial_inner(direction, applied), 'dev')  77 us
    gather x12, local copies, waits for them, and re-layouts, gather_faces(): return jnp.take(padded, inverse, axis=1)  70.2 us
    ppermute x36, starting transfers between devices, from_behind(): lax.ppermute(value, axis, [(i, (i + by) % length) for i in range(length)])  69.4 us
    dot_general x4, matrix products, dual_apply(): lax.dot_general(vector.astype(jnp.bfloat16), dual_blocks[0], (((1,), (1,)...  47.9 us
    all_gather x1, blocking collectives, per_device(): lax.all_gather(block_row.reshape(MODES, devices * MODES), 'dev', axis=0,...  39.5 us
  transfers between devices with their start and end apart: 36, of which 2 were waited for; matrix products, arithmetic and copies ran while one was open for 4% of the time, Pallas kernels for 0%

commit v1 on v0

v1 whole, which is shorter than its diff:
```python
import functools

import jax
import jax.numpy as jnp
from jax import lax
from jax.experimental import pallas as pl
from jax.experimental.pallas import tpu as pltpu
from jax.sharding import PartitionSpec as P

FACES = 6
MODES = 6
ITERS = 3
LANES = 128
ROWS = 256
FACE_STEPS = (-1, 1, -4, 4, -16, 16)
HIGHEST = lax.Precision.HIGHEST


def params(steps=None):
    if steps is None:
        return pltpu.CompilerParams(vmem_limit_bytes=50 * 2**20)
    return pltpu.CompilerParams(
        dimension_semantics=("arbitrary",), vmem_limit_bytes=50 * 2**20
    )


def gather_lanes(source, index_ref, block):
    index = jnp.broadcast_to(index_ref[pl.ds(block, 1), :], (source.shape[0], LANES))
    low = jnp.bitwise_and(index, LANES - 1)
    high = jnp.right_shift(index, 7)
    picked = jnp.zeros((source.shape[0], LANES), jnp.float32)
    for part in range(source.shape[1] // LANES):
        taken = jnp.take_along_axis(
            source[:, part * LANES : (part + 1) * LANES], low, axis=1, mode="promise_in_bounds"
        )
        picked = jnp.where(high == part, taken, picked)
    return picked


def setup_kernel(codes_ref, values_ref, modes_ref, rhs_ref, inverse_ref, onehot_ref, left_ref):
    codes = codes_ref[...]
    nmax = codes.shape[1]
    blocks = nmax // LANES
    wide = left_ref.shape[0] // 3
    columns = lax.broadcasted_iota(jnp.int32, (1, nmax), 1)
    high = jnp.right_shift(codes, 7)
    low = jnp.where(codes < 0, -1, jnp.bitwise_and(codes, LANES - 1))
    rows = lax.broadcasted_iota(jnp.int32, (LANES, nmax), 0)
    onehot_ref[...] = jnp.where(rows == low, 1.0, 0.0).astype(jnp.bfloat16)
    hit = lax.broadcasted_iota(jnp.int32, (wide, nmax), 0) == high
    upper = jnp.right_shift(columns, 7).astype(jnp.float32)
    lower = jnp.bitwise_and(columns, LANES - 1).astype(jnp.float32)
    left_ref[:wide, :] = jnp.where(hit, upper, 0.0).astype(jnp.bfloat16)
    left_ref[wide : 2 * wide, :] = jnp.where(hit, lower, 0.0).astype(jnp.bfloat16)
    left_ref[2 * wide :, :] = jnp.where(hit, 1.0, 0.0).astype(jnp.bfloat16)
    found = lax.dot_general(
        left_ref[...], onehot_ref[...], (((1,), (1,)), ((), ())),
        preferred_element_type=jnp.float32,
    )
    place = found[:wide] * LANES + found[wide : 2 * wide]
    place = jnp.where(found[2 * wide :] > 0.5, place, float(nmax))
    inverse_ref[...] = (place[:blocks] + 0.5).astype(jnp.int32)

    def body(block, carry):
        start = pl.multiple_of(block * LANES, LANES)
        modes_ref[:, pl.ds(start, LANES)] = gather_lanes(values_ref.at[0], inverse_ref, block)
        rhs_ref[:, pl.ds(start, LANES)] = gather_lanes(values_ref.at[1], inverse_ref, block)
        return carry

    lax.fori_loop(0, blocks, body, 0)


def invert_kernel(matrix_ref, out_ref):
    size, width = out_ref.shape
    out_ref[...] = matrix_ref[...]
    lane = lax.broadcasted_iota(jnp.int32, (1, width), 1)

    def body(step, carry):
        k = 2 * step
        at0, at1 = lane == k, lane == k + 1
        row0 = out_ref[pl.ds(k, 1), :]
        row1 = out_ref[pl.ds(k + 1, 1), :]
        p00 = jnp.sum(jnp.where(at0, row0, 0.0), axis=1, keepdims=True)
        p01 = jnp.sum(jnp.where(at1, row0, 0.0), axis=1, keepdims=True)
        p11 = jnp.sum(jnp.where(at1, row1, 0.0), axis=1, keepdims=True)
        first = 1.0 / p00
        ratio = p01 * first
        i11 = 1.0 / (p11 - p01 * ratio)
        i01 = -ratio * i11
        i00 = first + ratio * ratio * i11
        use0 = i00 * row0 + i01 * row1
        use1 = i01 * row0 + i11 * row1
        whole = out_ref[...]
        col0 = jnp.sum(jnp.where(at0, whole, 0.0), axis=1, keepdims=True)
        col1 = jnp.sum(jnp.where(at1, whole, 0.0), axis=1, keepdims=True)
        fresh = whole - col0 * use0 - col1 * use1
        fresh = jnp.where(at0, col0 * i00 + col1 * i01, fresh)
        fresh = jnp.where(at1, col0 * i01 + col1 * i11, fresh)
        out_ref[...] = fresh
        out_ref[pl.ds(k, 1), :] = jnp.where(at0, -i00, jnp.where(at1, -i01, use0))
        out_ref[pl.ds(k + 1, 1), :] = jnp.where(at0, -i01, jnp.where(at1, -i11, use1))
        return carry

    lax.fori_loop(0, size // 2, body, 0)
    out_ref[...] = -out_ref[...]


def coarse_apply(coarse, picks_ref, modes_ref, far_ref, cap):
    z = lax.dot_general(
        coarse, picks_ref[...], (((1,), (0,)), ((), ())),
        precision=HIGHEST, preferred_element_type=jnp.float32,
    )
    blocks = []
    for face in range(FACES):
        span = slice(face * cap, (face + 1) * cap)
        total = jnp.zeros((coarse.shape[0], cap), jnp.float32)
        for mode in range(MODES):
            total += z[:, mode : mode + 1] * modes_ref[mode : mode + 1, span]
            column = (face + 1) * MODES + mode
            total -= z[:, column : column + 1] * far_ref[mode : mode + 1, span]
        blocks.append(total)
    return blocks


def product_steps(step, steps, vector_ref, map_ref, inverse_ref, dual_ref, sum_ref, outs, cap):
    per_step = dual_ref.shape[1] // LANES
    pieces = [gather_lanes(vector_ref, map_ref, step * per_step + i) for i in range(per_step)]
    vector = jnp.concatenate(pieces, axis=1).astype(jnp.bfloat16)
    part = jnp.dot(vector, dual_ref[0], preferred_element_type=jnp.float32)

    @pl.when(step == 0)
    def _():
        sum_ref[...] = part

    @pl.when(step > 0)
    def _():
        sum_ref[...] += part

    @pl.when(step == steps - 1)
    def _():
        def body(block, carry):
            start = pl.multiple_of(block * LANES, LANES)
            for face in range(FACES):
                outs[face][:, pl.ds(start, LANES)] = gather_lanes(
                    sum_ref, inverse_ref, face * (cap // LANES) + block
                )
            return carry

        lax.fori_loop(0, cap // LANES, body, 0)


def start_kernel(
    steps, cap, coarse_ref, picks_ref, modes_ref, far_ref, map_ref, inverse_ref, dual_ref,
    mult_ref, *rest,
):
    outs, sum_ref = rest[:FACES], rest[FACES]
    step = pl.program_id(0)

    @pl.when(step == 0)
    def _():
        parts = coarse_apply(coarse_ref[...], picks_ref, modes_ref, far_ref, cap)
        for face, part in enumerate(parts):
            mult_ref[:, face * cap : (face + 1) * cap] = part

    product_steps(step, steps, mult_ref, map_ref, inverse_ref, dual_ref, sum_ref, outs, cap)


def first_kernel(
    steps, cap, gathered_ref, picks_ref, modes_ref, far_ref, residual_ref, map_ref, inverse_ref,
    dual_ref, w_ref, *rest,
):
    outs, sum_ref = rest[:FACES], rest[FACES]
    step = pl.program_id(0)

    @pl.when(step == 0)
    def _():
        coarse = jnp.sum(gathered_ref[...], axis=0)
        parts = coarse_apply(coarse, picks_ref, modes_ref, far_ref, cap)
        for face, part in enumerate(parts):
            span = slice(face * cap, (face + 1) * cap)
            w_ref[:, span] = residual_ref[:, span] - part

    product_steps(step, steps, w_ref, map_ref, inverse_ref, dual_ref, sum_ref, outs, cap)


def advance(
    cap, slots, gathered_ref, picks_ref, modes_ref, far_ref, state, applied_ref, scalars_ref, outs
):
    mult_ref, w_ref, d_ref, q_ref, s_ref = state
    mult_out, w_out, d_out, q_out, s_out, scalars_out = outs
    coarse = jnp.sum(gathered_ref[...], axis=0)
    base = slots * MODES
    rho, wa, wq, da = (coarse[:, base + i : base + i + 1] for i in range(4))
    rho_old, dq_old = scalars_ref[:, 0:1], scalars_ref[:, 1:2]
    beta = rho / rho_old
    dq = wa + beta * (wq + da) + beta * beta * dq_old
    alpha = rho / dq
    parts = coarse_apply(coarse, picks_ref, modes_ref, far_ref, cap)
    for face, part in enumerate(parts):
        span = slice(face * cap, (face + 1) * cap)
        applied = applied_ref[:, span]
        d = w_ref[:, span] + beta * d_ref[:, span]
        s = applied - part + beta * s_ref[:, span]
        mult_out[:, span] = mult_ref[:, span] + alpha * d
        w_out[:, span] = w_ref[:, span] - alpha * s
        if d_out is not None:
            d_out[:, span] = d
            s_out[:, span] = s
            q_out[:, span] = applied + beta * q_ref[:, span]
    if scalars_out is not None:
        lane = lax.broadcasted_iota(jnp.int32, scalars_out.shape, 1)
        scalars_out[...] = jnp.where(lane == 0, rho, jnp.where(lane == 1, dq, 0.0))


def step_kernel(
    steps, cap, slots, gathered_ref, picks_ref, modes_ref, far_ref, m_ref, w_ref, d_ref, q_ref,
    s_ref, applied_ref, scalars_ref, map_ref, inverse_ref, dual_ref,
    m_out, w_out, d_out, q_out, s_out, scalars_out, *rest,
):
    outs, sum_ref = rest[:FACES], rest[FACES]
    step = pl.program_id(0)

    @pl.when(step == 0)
    def _():
        advance(
            cap, slots, gathered_ref, picks_ref, modes_ref, far_ref,
            (m_ref, w_ref, d_ref, q_ref, s_ref), applied_ref, scalars_ref,
            (m_out, w_out, d_out, q_out, s_out, scalars_out),
        )

    product_steps(step, steps, w_out, map_ref, inverse_ref, dual_ref, sum_ref, outs, cap)


def last_kernel(
    cap, slots, gathered_ref, picks_ref, modes_ref, far_ref, m_ref, w_ref, d_ref, q_ref, s_ref,
    applied_ref, scalars_ref, map_ref, m_out, w_out, m_tmp, w_tmp,
):
    advance(
        cap, slots, gathered_ref, picks_ref, modes_ref, far_ref,
        (m_ref, w_ref, d_ref, q_ref, s_ref), applied_ref, scalars_ref,
        (m_tmp, w_tmp, None, None, None, None),
    )

    def body(block, carry):
        start = pl.multiple_of(block * LANES, LANES)
        m_out[0, :, pl.ds(start, LANES)] = gather_lanes(m_tmp, map_ref, block)
        w_out[0, :, pl.ds(start, LANES)] = gather_lanes(w_tmp, map_ref, block)
        return carry

    lax.fori_loop(0, m_tmp.shape[1] // LANES, body, 0)


def combine_kernel(cap, slots, initial, slot_ref, modes_ref, masks_ref, *rest):
    own, far, rest = rest[:FACES], rest[FACES : 2 * FACES], rest[2 * FACES :]
    if initial:
        rhs_ref, rhs_far_ref, out_ref, sums_ref = rest
    else:
        w_ref, d_ref, q_ref, out_ref, sums_ref = rest
    loads = own[0].shape[0]
    counts = MODES if initial else MODES + 4
    totals = [jnp.zeros((loads, cap), jnp.float32) for _ in range(counts)]
    for face in range(FACES):
        span = slice(face * cap, (face + 1) * cap)
        shared = masks_ref[0:1, span]
        value = own[face][...] - shared * far[face][...]
        if initial:
            value = rhs_ref[:, span] - shared * rhs_far_ref[:, span] - value
        out_ref[:, span] = value
        for mode in range(MODES):
            totals[mode] += value * modes_ref[mode : mode + 1, span]
        if not initial:
            weights = masks_ref[1:2, span]
            weighted_w = weights * w_ref[:, span]
            totals[MODES] += weighted_w * w_ref[:, span]
            totals[MODES + 1] += weighted_w * value
            totals[MODES + 2] += weighted_w * q_ref[:, span]
            totals[MODES + 3] += weights * d_ref[:, span] * value
    lane = lax.broadcasted_iota(jnp.int32, sums_ref.shape, 1)
    result = jnp.zeros(sums_ref.shape, jnp.float32)
    for index, total in enumerate(totals):
        place = slot_ref[0] * MODES + index if index < MODES else slots * MODES + index - MODES
        result = jnp.where(lane == place, jnp.sum(total, axis=1, keepdims=True), result)
    sums_ref[...] = result


def per_device(
    dual_blocks, rigid_modes, dual_local, coarse_rhs, iface_sizes, neighbours, shared_counts,
    iface_map, owner,
):
    my_slot = lax.axis_index("dev")
    slots = lax.axis_size("dev")
    loads, nmax = dual_local.shape[1:]
    cap = nmax // FACES
    blocks = nmax // LANES
    size = slots * MODES
    width = -(-(size + 4) // LANES) * LANES
    steps = nmax // ROWS
    f32 = jnp.float32
    shape = jax.ShapeDtypeStruct
    vector, face_vec = shape((loads, nmax), f32), shape((loads, cap), f32)
    scalar_shape, sums_shape = shape((loads, LANES), f32), shape((loads, width), f32)

    live = jnp.arange(nmax, dtype=jnp.int32) < iface_sizes[0]
    codes = jnp.where(live, iface_map[0], -1)
    code_table = codes.reshape(blocks, LANES)
    padded = jnp.pad(rigid_modes[0], ((0, loads - MODES), (0, 0)))
    modes, rhs, inverse = pl.pallas_call(
        setup_kernel,
        out_shape=(vector, vector, shape((blocks, LANES), jnp.int32)),
        scratch_shapes=[
            pltpu.VMEM((LANES, nmax), jnp.bfloat16),
            pltpu.VMEM((3 * 32, nmax), jnp.bfloat16),
        ],
        compiler_params=params(),
    )(codes.reshape(1, nmax), jnp.stack([padded, dual_local[0]]))

    def exchange(pieces):
        return [
            lax.ppermute(
                pieces[face ^ 1], "dev",
                [(i, (i - FACE_STEPS[face]) % slots) for i in range(slots)],
            )
            for face in range(FACES)
        ]

    both = jnp.concatenate([modes, rhs], axis=0)
    far_pieces = exchange([both[:, f * cap : (f + 1) * cap] for f in range(FACES)])
    position = jnp.arange(cap, dtype=jnp.int32)
    counted = position[None, :] < shared_counts[0][:, None]
    shared = (counted & (neighbours[0] >= 0)[:, None]).astype(f32).reshape(1, nmax)
    weights = counted.astype(f32).reshape(1, nmax) - 0.5 * shared
    masks = jnp.concatenate([shared, weights, jnp.zeros((6, nmax), f32)], axis=0)
    far_both = jnp.concatenate(far_pieces, axis=1) * shared
    far_modes, far_rhs = far_both[:loads], far_both[loads:]

    own6 = modes[:MODES].reshape(MODES, FACES, cap)
    far6 = far_modes[:MODES].reshape(MODES, FACES, cap)
    diagonal = lax.dot_general(
        modes[:MODES], modes[:MODES], (((1,), (1,)), ((), ())), precision=HIGHEST
    )
    coupling = -jnp.einsum("afp,bfp->fab", own6, far6, precision=HIGHEST)
    ids = jnp.arange(slots, dtype=jnp.int32)
    row = jnp.where((ids == my_slot)[None, :, None], diagonal[:, None, :], 0.0)
    for face in range(FACES):
        target = (my_slot + FACE_STEPS[face]) % slots
        row += jnp.where((ids == target)[None, :, None], coupling[face][:, None, :], 0.0)
    row = row.reshape(MODES, size)
    row = jnp.concatenate(
        [row, jnp.pad(coarse_rhs[0], ((0, 0), (0, width - size - loads)))]
        if width - size >= loads
        else [row, jnp.pad(coarse_rhs[0], ((0, 0), (0, LANES - loads)))],
        axis=1,
    )
    everything = lax.all_gather(row, "dev", axis=0, tiled=True)
    goal = jnp.pad(everything[:, size : size + loads].T, ((0, 0), (0, width - size)))
    matrix = jnp.pad(everything[:, :size], ((0, 0), (0, width - size)))
    inverted = pl.pallas_call(
        invert_kernel,
        out_shape=shape((size, width), f32),
        compiler_params=params(),
    )(matrix)
    groups = [
        lax.dynamic_slice(inverted, (((my_slot + by) % slots) * MODES, 0), (MODES, width))
        for by in (0,) + FACE_STEPS
    ]
    picks = jnp.pad(
        jnp.concatenate(groups, axis=0), ((0, LANES - MODES * (FACES + 1)), (0, 0))
    ).T
    picks = jnp.where((jnp.arange(width) < size)[:, None], picks, 0.0)

    def whole(item):
        return pl.BlockSpec(item.shape, lambda i, rank=len(item.shape): (0,) * rank)

    def with_product(kernel, ins, outs, *static):
        out_shape = tuple(outs) + (face_vec,) * FACES
        return pl.pallas_call(
            functools.partial(kernel, steps, cap, *static),
            grid=(steps,),
            in_specs=[whole(x) for x in ins]
            + [pl.BlockSpec((1, ROWS, nmax), lambda i: (0, i, 0))],
            out_specs=tuple(whole(x) for x in out_shape),
            out_shape=out_shape,
            scratch_shapes=[pltpu.VMEM((loads, nmax), f32)],
            compiler_params=params(steps),
        )(*ins, dual_blocks)

    slot_array = my_slot.reshape(1).astype(jnp.int32)

    def combine(own, extra, initial):
        far = exchange(own)
        ins = (modes, masks, *own, *far, *extra)
        value, sums = pl.pallas_call(
            functools.partial(combine_kernel, cap, slots, initial),
            in_specs=[pl.BlockSpec(memory_space=pltpu.SMEM)]
            + [pl.BlockSpec(memory_space=pltpu.VMEM)] * len(ins),
            out_shape=(vector, sums_shape),
            compiler_params=params(),
        )(slot_array, *ins)
        return value, lax.all_gather(sums, "dev", axis=0)

    mult, *own = with_product(
        start_kernel, (goal, picks, modes, far_modes, code_table, inverse), (vector,)
    )
    residual, gathered = combine(own, (rhs, far_rhs), True)
    w, *own = with_product(
        first_kernel, (gathered, picks, modes, far_modes, residual, code_table, inverse), (vector,)
    )
    d = q = s = jnp.zeros((loads, nmax), f32)
    scalars = jnp.broadcast_to(
        jnp.where(jnp.arange(LANES) == 0, 1.0, 0.0).astype(f32), (loads, LANES)
    )
    for step in range(ITERS):
        applied, gathered = combine(own, (w, d, q), False)
        ins = (gathered, picks, modes, far_modes, mult, w, d, q, s, applied, scalars, code_table)
        if step < ITERS - 1:
            mult, w, d, q, s, scalars, *own = with_product(
                step_kernel, ins + (inverse,), (vector,) * 5 + (scalar_shape,), slots
            )
    return pl.pallas_call(
        functools.partial(last_kernel, cap, slots),
        out_shape=(shape((1, loads, nmax), f32),) * 2,
        scratch_shapes=[pltpu.VMEM((loads, nmax), f32)] * 2,
        compiler_params=params(),
    )(*ins)


def solution(mesh):
    return jax.shard_map(
        per_device,
        mesh=mesh,
        in_specs=(
            P("dev", None, None),
            P("dev", None, None),
            P("dev", None, None),
            P("dev", None, None),
            P("dev"),
            P("dev", None),
            P("dev", None),
            P("dev", None),
            P(),
        ),
        out_specs=(P("dev", None, None), P("dev", None, None)),
        check_vma=False,
    )
```

time: 954 us -> 338 us (0.35)
  local copies, waits for them, and re-layouts: 283 us -> 4.68 us
  blocking collectives: 429 us -> 201 us
  matrix products: 80.1 us -> 0.54 us
  Pallas kernels: 0 us -> 77.9 us
  other arithmetic: 72 us -> 4.89 us
  starting transfers between devices: 69.4 us -> 34.3 us
    psum x9 -> x0, blocking collectives: 353 us -> none  [the longest x4 156 us: project(): coarse_all = lax.psum(placed, 'dev').reshape(devices * MODES, loads)]
    gather x38 -> x0, local copies, waits for them, and re-layouts: 213 us -> none  [the longest x20 139 us: spread_back(): return jnp.take(flattened, dof_codes, axis=1) * shared_float[None]]
    all_gather x2 -> x5, blocking collectives: 76 us -> 201 us  [the longest x4 162 us: combine(): return (value, lax.all_gather(sums, 'dev', axis=0))]
    pallas_call x0 -> x11, Pallas kernels: none -> 77.9 us  [the longest x4 53.3 us: with_product(): pl.pallas_call(functools.partial(kernel, steps, cap, *static), grid=(step...]
    dot_general x20 -> x2, matrix products: 68.8 us -> 0.54 us  [the longest x1 0.28 us: per_device(): coupling = -jnp.einsum('afp,bfp->fab', own6, far6, precision=HIGHEST)]
    another operation x20 -> x1, other arithmetic: 50.8 us -> 0.91 us  [per_device(): jnp.stack([padded, dual_local[0]])]
    ppermute x36 -> x30, starting transfers between devices: 69.4 us -> 34.3 us  [exchange(): lax.ppermute(pieces[face ^ 1], 'dev', [(i, (i - FACE_STEPS[face]) % slots...]
    unnamed x203 -> x14, local copies, waits for them, and re-layouts: 27.1 us -> 1.75 us
  transfers between devices with their start and end apart: 36 -> 30, of which waited for: 2 -> 18; matrix products, arithmetic and copies ran while one was open for 4% -> 1% of each run, Pallas kernels for 0% -> 0%
where the time goes in v1:
time: 338 us; the launch traced here: 337 us
  blocking collectives  201 us (59%)
  Pallas kernels  77.9 us (23%)
  starting transfers between devices  34.3 us (10%)
  waiting for transfers between devices  12.7 us (4%)
  other arithmetic  4.89 us (1%)
  local copies, waits for them, and re-layouts  4.68 us (1%)
    all_gather x4, blocking collectives, combine(): return (value, lax.all_gather(sums, 'dev', axis=0))  162 us
    pallas_call x4, Pallas kernels, with_product(): pl.pallas_call(functools.partial(kernel, steps, cap, *static), grid=(step...  53.3 us
    all_gather x1, blocking collectives, per_device(): everything = lax.all_gather(row, 'dev', axis=0, tiled=True)  39 us
    ppermute x30, starting transfers between devices, exchange(): lax.ppermute(pieces[face ^ 1], 'dev', [(i, (i - FACE_STEPS[face]) % slots...  34.3 us
    pallas_call x1, Pallas kernels, per_device(): pl.pallas_call(invert_kernel, out_shape=shape((size, width), f32), compil...  16.5 us
    ppermute x30, waiting for transfers between devices, exchange(): lax.ppermute(pieces[face ^ 1], 'dev', [(i, (i - FACE_STEPS[face]) % slots...  12.7 us
  transfers between devices with their start and end apart: 30, of which 18 were waited for; matrix products, arithmetic and copies ran while one was open for 1% of the time, Pallas kernels for 0%

profile of v1, /device:TPU:0, one launch (start us, length us, event | category | flops | bytes accessed | tf_op | source)
XLA Modules:
  0.0 337.5 jit_solution(11642547290808215875)
XLA Ops:
  1.3 0.9 copy.49
  2.2 0.7 compare_select_fusion.codes_ref
  3.0 0.9 pad_maximum_fusion.values_ref
  3.9 3.5 %shard_map.95 = (f32[8,3072]{1,0:T(8,128)S(1)}, f32[8,3072]{1,0:T(8,128)S(1)}, s32[24,128]{1,0:T(8,128)S(1)}) custom-call(s32[1,3072]{1,0:T(1,128)S(1)} %compare_select_fusion.codes_ref, f32[2,8,3072]{2,1,0:T(8,128)S(1)} %pad_maximum_fusion.values_ref), custom_call_target="tpu_custom_call" | custom-call | tf_op jit(solution)/shard_map/pallas_call | solution.py:307
  7.4 4.1 %collective-permute-start.5 = (f32[16,512]{1,0:T(8,128)S(1)}, f32[16,512]{1,0:T(8,128)S(1)}, u32[]{:S(2)}, u32[]{:S(2)}) collective-permute-start(f32[16,512]{1,0:T(8,128)S(1)} %get-tuple-element.109), channel_id=1, source_target_pairs={{0,16},{1,17},{2,18},{3,19},{4,20},{5,21},{6,22},{7,23},{8,24},{9,... | collective-permute-start | bytes 98312 | tf_op jit(solution)/shard_map/ppermute | solution.py:319
  11.6 4.8 %collective-permute-start.3 = (f32[16,512]{1,0:T(8,128)S(1)}, f32[16,512]{1,0:T(8,128)S(1)}, u32[]{:S(2)}, u32[]{:S(2)}) collective-permute-start(f32[16,512]{1,0:T(8,128)S(1)} %get-tuple-element.111), channel_id=1, source_target_pairs={{0,28},{1,29},{2,30},{3,31},{4,0},{5,1},{6,2},{7,3},{8,4},{9,5},{1... | collective-permute-start | bytes 98312 | tf_op jit(solution)/shard_map/ppermute | solution.py:319
  16.8 0.7 compare_bitcast_fusion
  17.5 0.7 fusion.2.map_ref
  18.2 0.7 fusion.1
  20.4 0.7 copy.50
  21.2 2.2 collective-permute-done
  23.4 3.2 collective-permute-start.1
  26.6 1.6 collective-permute-done.1
  28.4 0.3 convolution_negate_fusion
  29.5 39.0 %all-gather.4 = f32[32,6,256]{2,1,0:T(8,128)S(1)} all-gather(f32[1,6,256]{2,1,0:T(8,128)S(1)} %fusion.3), channel_id=1, replica_groups=mesh['dev'=32] {'dev'}, dimensions={0}, use_global_device_ids=true | all-gather | bytes 202752 | tf_op jit(solution)/shard_map/all_gather | solution.py:354
  68.7 0.7 broadcast_select_fusion.matrix_ref
  69.4 16.5 %shard_map.96 = f32[192,256]{1,0:T(8,128)S(1)} custom-call(f32[192,256]{1,0:T(8,128)S(1)} %broadcast_select_fusion.matrix_ref), custom_call_target="tpu_custom_call" | custom-call | tf_op jit(solution)/shard_map/pallas_call | solution.py:357
  86.0 0.4 concatenate.19
  86.6 13.3 %shard_map.97 = (f32[8,3072]{1,0:T(8,128)S(1)}, f32[8,512]{1,0:T(8,128)S(1)}, f32[8,512]{1,0:T(8,128)S(1)}, f32[8,512]{1,0:T(8,128)S(1)}, f32[8,512]{1,0:T(8,128...) custom-call(f32[8,256]{1,0:T(8,128)S(1)} %pad.22.coarse_ref, f32[256,128]{1,0:T(8,128)S(1)} %select_bitcast_fusion.picks_ref, ...), custom_call_target="tpu_custom_call" | custom-call | tf_op jit(solution)/shard_map/pallas_call | solution.py:376
  100.2 0.5 collective-permute-start.6
  100.6 2.0 collective-permute-start.8
  102.7 2.9 collective-permute-start.10
  105.7 1.3 collective-permute-done.6.rest_6_
  107.2 0.6 collective-permute-done.11.rest_11_
  107.8 0.4 collective-permute-done.10.rest_10_
  108.2 40.4 %all-gather = f32[256,256]{1,0:T(8,128)S(1)} all-gather(f32[8,256]{1,0:T(8,128)S(1)} %get-tuple-element.60), channel_id=2, replica_groups=mesh['dev'=32] {'dev'}, dimensions={0}, use_global_device_ids=true | all-gather | bytes 270336 | tf_op jit(solution)/shard_map/all_gather | solution.py:399
  148.7 13.3 %shard_map.99 = (f32[8,3072]{1,0:T(8,128)S(1)}, f32[8,512]{1,0:T(8,128)S(1)}, f32[8,512]{1,0:T(8,128)S(1)}, f32[8,512]{1,0:T(8,128)S(1)}, f32[8,512]{1,0:T(8,128...) custom-call(f32[32,8,256]{2,1,0:T(8,128)S(1)} %bitcast.53, f32[256,128]{1,0:T(8,128)S(1)} %select_bitcast_fusion.picks_ref, ...), custom_call_target="tpu_custom_call" | custom-call | tf_op jit(solution)/shard_map/pallas_call | solution.py:376
  162.0 0.5 collective-permute-start.12
  162.5 2.0 collective-permute-start.14
  164.6 2.9 collective-permute-start.16
  167.5 1.4 collective-permute-done.12.rest_6_
  169.3 0.4 collective-permute-done.16.rest_10_
  169.8 40.4 %all-gather.1 = f32[256,256]{1,0:T(8,128)S(1)} all-gather(f32[8,256]{1,0:T(8,128)S(1)} %get-tuple-element.69), channel_id=3, replica_groups=mesh['dev'=32] {'dev'}, dimensions={0}, use_global_device_ids=true | all-gather | bytes 270336 | tf_op jit(solution)/shard_map/all_gather | solution.py:399
  210.2 13.4 %shard_map.101 = (f32[8,3072]{1,0:T(8,128)S(1)}, f32[8,3072]{1,0:T(8,128)S(1)}, f32[8,3072]{1,0:T(8,128)S(1)}, f32[8,3072]{1,0:T(8,128)S(1)}, f32[8,3072]{1,0:T(...) custom-call(f32[32,8,256]{2,1,0:T(8,128)S(1)} %bitcast.52, ...), custom_call_target="tpu_custom_call" | custom-call | tf_op jit(solution)/shard_map/pallas_call | solution.py:376
  223.6 0.5 collective-permute-start.18
  224.1 2.0 collective-permute-start.20
  226.2 2.9 collective-permute-start.22
  229.1 1.4 collective-permute-done.18.rest_6_
  230.9 0.4 collective-permute-done.22.rest_10_
  231.4 40.4 %all-gather.2 = f32[256,256]{1,0:T(8,128)S(1)} all-gather(f32[8,256]{1,0:T(8,128)S(1)} %get-tuple-element.81), channel_id=4, replica_groups=mesh['dev'=32] {'dev'}, dimensions={0}, use_global_device_ids=true | all-gather | bytes 270336 | tf_op jit(solution)/shard_map/all_gather | solution.py:399
  271.8 13.4 %shard_map.103 = (f32[8,3072]{1,0:T(8,128)S(1)}, f32[8,3072]{1,0:T(8,128)S(1)}, f32[8,3072]{1,0:T(8,128)S(1)}, f32[8,3072]{1,0:T(8,128)S(1)}, f32[8,3072]{1,0:T(...) custom-call(f32[32,8,256]{2,1,0:T(8,128)S(1)} %bitcast.51, ...), custom_call_target="tpu_custom_call" | custom-call | tf_op jit(solution)/shard_map/pallas_call | solution.py:376
  285.2 0.5 collective-permute-start.24
  285.7 2.0 collective-permute-start.26
  287.8 2.9 collective-permute-start.28
  290.7 1.4 collective-permute-done.24.rest_6_
  292.5 0.4 collective-permute-done.28.rest_10_
  293.0 40.4 %all-gather.3 = f32[256,256]{1,0:T(8,128)S(1)} all-gather(f32[8,256]{1,0:T(8,128)S(1)} %get-tuple-element.95), channel_id=5, replica_groups=mesh['dev'=32] {'dev'}, dimensions={0}, use_global_device_ids=true | all-gather | bytes 270336 | tf_op jit(solution)/shard_map/all_gather | solution.py:399
  333.4 4.1 %shard_map.105 = (f32[1,8,3072]{2,1,0:T(8,128)}, f32[1,8,3072]{2,1,0:T(8,128)}) custom-call(f32[32,8,256]{2,1,0:T(8,128)S(1)} %bitcast.54, f32[256,128]{1,0:T(8,128)S(1)} %select_bitcast_fusion.picks_ref, f32[8,3072]{1,0:T(8,128)S(1)} %get-tuple-element.51.modes_ref, f32[8,3072]{1,0:T(8,128)S(1)} %get-tuple-element.101.far_ref, ...), custom_call_target="tpu_custom_call" | custom-call | tf_op jit(solution)/shard_map/pallas_call | solution.py:419
  (110 shorter events, 6.0 us)
Async XLA Ops:
  0.6 99.3 %copy-start = (s32[1,6]{1,0:T(1,128)S(1)}, s32[1,6]{1,0:T(1,128)}, u32[]{:S(2)}) copy-start(s32[1,6]{1,0:T(1,128)} %param.15) | copy-start | bytes 76
  7.4 20.9 %collective-permute-start.5 = (f32[16,512]{1,0:T(8,128)S(1)}, f32[16,512]{1,0:T(8,128)S(1)}, u32[]{:S(2)}, u32[]{:S(2)}) collective-permute-start(f32[16,512]{1,0:T(8,128)S(1)} %get-tuple-element.109), channel_id=1, source_target_pairs={{0,16},{1,17},{2,18},{3,19},{4,20},{5,21},{6,22},{7,23},{8,24},{9,... | collective-permute-start | bytes 98312 | tf_op jit(solution)/shard_map/ppermute | solution.py:319
  11.5 16.7 %collective-permute-start.4 = (f32[16,512]{1,0:T(8,128)S(1)}, f32[16,512]{1,0:T(8,128)S(1)}, u32[]{:S(2)}, u32[]{:S(2)}) collective-permute-start(f32[16,512]{1,0:T(8,128)S(1)} %get-tuple-element.110), channel_id=1, source_target_pairs={{0,16},{1,17},{2,18},{3,19},{4,20},{5,21},{6,22},{7,23},{8,24},{9,... | collective-permute-start | bytes 98312 | tf_op jit(solution)/shard_map/ppermute | solution.py:319
  11.6 16.6 %collective-permute-start.3 = (f32[16,512]{1,0:T(8,128)S(1)}, f32[16,512]{1,0:T(8,128)S(1)}, u32[]{:S(2)}, u32[]{:S(2)}) collective-permute-start(f32[16,512]{1,0:T(8,128)S(1)} %get-tuple-element.111), channel_id=1, source_target_pairs={{0,28},{1,29},{2,30},{3,31},{4,0},{5,1},{6,2},{7,3},{8,4},{9,5},{1... | collective-permute-start | bytes 98312 | tf_op jit(solution)/shard_map/ppermute | solution.py:319
  16.4 11.8 %collective-permute-start.2 = (f32[16,512]{1,0:T(8,128)S(1)}, f32[16,512]{1,0:T(8,128)S(1)}, u32[]{:S(2)}, u32[]{:S(2)}) collective-permute-start(f32[16,512]{1,0:T(8,128)S(1)} %get-tuple-element.112), channel_id=1, source_target_pairs={{0,4},{1,5},{2,6},{3,7},{4,8},{5,9},{6,10},{7,11},{8,12},{9,13},{1... | collective-permute-start | bytes 98312 | tf_op jit(solution)/shard_map/ppermute | solution.py:319
  16.4 7.0 %collective-permute-start = (f32[16,512]{1,0:T(8,128)S(1)}, f32[16,512]{1,0:T(8,128)S(1)}, u32[]{:S(2)}, u32[]{:S(2)}) collective-permute-start(f32[16,512]{1,0:T(8,128)S(1)} %get-tuple-element.114), channel_id=1, source_target_pairs={{0,1},{1,2},{2,3},{3,4},{4,5},{5,6},{6,7},{7,8},{8,9},{9,10},{10,1... | collective-permute-start | bytes 98312 | tf_op jit(solution)/shard_map/ppermute | solution.py:319
  23.4 4.8 %collective-permute-start.1 = (f32[16,512]{1,0:T(8,128)S(1)}, f32[16,512]{1,0:T(8,128)S(1)}, u32[]{:S(2)}, u32[]{:S(2)}) collective-permute-start(f32[16,512]{1,0:T(8,128)S(1)} %get-tuple-element.113), channel_id=1, source_target_pairs={{0,31},{1,0},{2,1},{3,2},{4,3},{5,4},{6,5},{7,6},{8,7},{9,8},{10,9... | collective-permute-start | bytes 98312 | tf_op jit(solution)/shard_map/ppermute | solution.py:319
  99.9 2.8 collective-permute-start.7
  100.2 6.8 %collective-permute-start.6 = (f32[8,512]{1,0:T(8,128)S(1)}, f32[8,512]{1,0:T(8,128)S(1)}, u32[]{:S(2)}, u32[]{:S(2)}) collective-permute-start(f32[8,512]{1,0:T(8,128)S(1)} %get-tuple-element.55.rest_1_), channel_id=1, source_target_pairs={{0,1},{1,2},{2,3},{3,4},{4,5},{5,6},{6,7},{7,8},{8,9},{9,10},{10,1... | collective-permute-start | bytes 49160 | tf_op jit(solution)/shard_map/ppermute | solution.py:319
  100.6 6.3 %collective-permute-start.9 = (f32[8,512]{1,0:T(8,128)S(1)}, f32[8,512]{1,0:T(8,128)S(1)}, u32[]{:S(2)}, u32[]{:S(2)}) collective-permute-start(f32[8,512]{1,0:T(8,128)S(1)} %get-tuple-element.56.rest_2_), channel_id=1, source_target_pairs={{0,28},{1,29},{2,30},{3,31},{4,0},{5,1},{6,2},{7,3},{8,4},{9,5},{1... | collective-permute-start | bytes 49160 | tf_op jit(solution)/shard_map/ppermute | solution.py:319
  100.6 6.5 %collective-permute-start.8 = (f32[8,512]{1,0:T(8,128)S(1)}, f32[8,512]{1,0:T(8,128)S(1)}, u32[]{:S(2)}, u32[]{:S(2)}) collective-permute-start(f32[8,512]{1,0:T(8,128)S(1)} %get-tuple-element.57.rest_3_), channel_id=1, source_target_pairs={{0,4},{1,5},{2,6},{3,7},{4,8},{5,9},{6,10},{7,11},{8,12},{9,13},{1... | collective-permute-start | bytes 49160 | tf_op jit(solution)/shard_map/ppermute | solution.py:319
  102.7 5.1 %collective-permute-start.11 = (f32[8,512]{1,0:T(8,128)S(1)}, f32[8,512]{1,0:T(8,128)S(1)}, u32[]{:S(2)}, u32[]{:S(2)}) collective-permute-start(f32[8,512]{1,0:T(8,128)S(1)} %get-tuple-element.58.rest_4_), channel_id=1, source_target_pairs={{0,16},{1,17},{2,18},{3,19},{4,20},{5,21},{6,22},{7,23},{8,24},{9,... | collective-permute-start | bytes 49160 | tf_op jit(solution)/shard_map/ppermute | solution.py:319
  102.7 5.4 %collective-permute-start.10 = (f32[8,512]{1,0:T(8,128)S(1)}, f32[8,512]{1,0:T(8,128)S(1)}, u32[]{:S(2)}, u32[]{:S(2)}) collective-permute-start(f32[8,512]{1,0:T(8,128)S(1)} %get-tuple-element.59.rest_5_), channel_id=1, source_target_pairs={{0,16},{1,17},{2,18},{3,19},{4,20},{5,21},{6,22},{7,23},{8,24},{9,... | collective-permute-start | bytes 49160 | tf_op jit(solution)/shard_map/ppermute | solution.py:319
  162.0 2.6 collective-permute-start.13
  162.0 6.8 %collective-permute-start.12 = (f32[8,512]{1,0:T(8,128)S(1)}, f32[8,512]{1,0:T(8,128)S(1)}, u32[]{:S(2)}, u32[]{:S(2)}) collective-permute-start(f32[8,512]{1,0:T(8,128)S(1)} %get-tuple-element.63.rest_1_), channel_id=1, source_target_pairs={{0,1},{1,2},{2,3},{3,4},{4,5},{5,6},{6,7},{7,8},{8,9},{9,10},{10,1... | collective-permute-start | bytes 49160 | tf_op jit(solution)/shard_map/ppermute | solution.py:319
  162.5 6.3 %collective-permute-start.15 = (f32[8,512]{1,0:T(8,128)S(1)}, f32[8,512]{1,0:T(8,128)S(1)}, u32[]{:S(2)}, u32[]{:S(2)}) collective-permute-start(f32[8,512]{1,0:T(8,128)S(1)} %get-tuple-element.64.rest_2_), channel_id=1, source_target_pairs={{0,28},{1,29},{2,30},{3,31},{4,0},{5,1},{6,2},{7,3},{8,4},{9,5},{1... | collective-permute-start | bytes 49160 | tf_op jit(solution)/shard_map/ppermute | solution.py:319
  162.5 6.5 %collective-permute-start.14 = (f32[8,512]{1,0:T(8,128)S(1)}, f32[8,512]{1,0:T(8,128)S(1)}, u32[]{:S(2)}, u32[]{:S(2)}) collective-permute-start(f32[8,512]{1,0:T(8,128)S(1)} %get-tuple-element.65.rest_3_), channel_id=1, source_target_pairs={{0,4},{1,5},{2,6},{3,7},{4,8},{5,9},{6,10},{7,11},{8,12},{9,13},{1... | collective-permute-start | bytes 49160 | tf_op jit(solution)/shard_map/ppermute | solution.py:319
  164.6 4.8 %collective-permute-start.17 = (f32[8,512]{1,0:T(8,128)S(1)}, f32[8,512]{1,0:T(8,128)S(1)}, u32[]{:S(2)}, u32[]{:S(2)}) collective-permute-start(f32[8,512]{1,0:T(8,128)S(1)} %get-tuple-element.66.rest_4_), channel_id=1, source_target_pairs={{0,16},{1,17},{2,18},{3,19},{4,20},{5,21},{6,22},{7,23},{8,24},{9,... | collective-permute-start | bytes 49160 | tf_op jit(solution)/shard_map/ppermute | solution.py:319
  164.6 5.1 %collective-permute-start.16 = (f32[8,512]{1,0:T(8,128)S(1)}, f32[8,512]{1,0:T(8,128)S(1)}, u32[]{:S(2)}, u32[]{:S(2)}) collective-permute-start(f32[8,512]{1,0:T(8,128)S(1)} %get-tuple-element.67.rest_5_), channel_id=1, source_target_pairs={{0,16},{1,17},{2,18},{3,19},{4,20},{5,21},{6,22},{7,23},{8,24},{9,... | collective-permute-start | bytes 49160 | tf_op jit(solution)/shard_map/ppermute | solution.py:319
  223.6 2.6 collective-permute-start.19
  223.6 6.8 %collective-permute-start.18 = (f32[8,512]{1,0:T(8,128)S(1)}, f32[8,512]{1,0:T(8,128)S(1)}, u32[]{:S(2)}, u32[]{:S(2)}) collective-permute-start(f32[8,512]{1,0:T(8,128)S(1)} %get-tuple-element.73.rest_1_), channel_id=1, source_target_pairs={{0,1},{1,2},{2,3},{3,4},{4,5},{5,6},{6,7},{7,8},{8,9},{9,10},{10,1... | collective-permute-start | bytes 49160 | tf_op jit(solution)/shard_map/ppermute | solution.py:319
  224.1 6.3 %collective-permute-start.21 = (f32[8,512]{1,0:T(8,128)S(1)}, f32[8,512]{1,0:T(8,128)S(1)}, u32[]{:S(2)}, u32[]{:S(2)}) collective-permute-start(f32[8,512]{1,0:T(8,128)S(1)} %get-tuple-element.74.rest_2_), channel_id=1, source_target_pairs={{0,28},{1,29},{2,30},{3,31},{4,0},{5,1},{6,2},{7,3},{8,4},{9,5},{1... | collective-permute-start | bytes 49160 | tf_op jit(solution)/shard_map/ppermute | solution.py:319
  224.1 6.5 %collective-permute-start.20 = (f32[8,512]{1,0:T(8,128)S(1)}, f32[8,512]{1,0:T(8,128)S(1)}, u32[]{:S(2)}, u32[]{:S(2)}) collective-permute-start(f32[8,512]{1,0:T(8,128)S(1)} %get-tuple-element.75.rest_3_), channel_id=1, source_target_pairs={{0,4},{1,5},{2,6},{3,7},{4,8},{5,9},{6,10},{7,11},{8,12},{9,13},{1... | collective-permute-start | bytes 49160 | tf_op jit(solution)/shard_map/ppermute | solution.py:319
  226.2 4.8 %collective-permute-start.23 = (f32[8,512]{1,0:T(8,128)S(1)}, f32[8,512]{1,0:T(8,128)S(1)}, u32[]{:S(2)}, u32[]{:S(2)}) collective-permute-start(f32[8,512]{1,0:T(8,128)S(1)} %get-tuple-element.76.rest_4_), channel_id=1, source_target_pairs={{0,16},{1,17},{2,18},{3,19},{4,20},{5,21},{6,22},{7,23},{8,24},{9,... | collective-permute-start | bytes 49160 | tf_op jit(solution)/shard_map/ppermute | solution.py:319
  226.2 5.1 %collective-permute-start.22 = (f32[8,512]{1,0:T(8,128)S(1)}, f32[8,512]{1,0:T(8,128)S(1)}, u32[]{:S(2)}, u32[]{:S(2)}) collective-permute-start(f32[8,512]{1,0:T(8,128)S(1)} %get-tuple-element.77.rest_5_), channel_id=1, source_target_pairs={{0,16},{1,17},{2,18},{3,19},{4,20},{5,21},{6,22},{7,23},{8,24},{9,... | collective-permute-start | bytes 49160 | tf_op jit(solution)/shard_map/ppermute | solution.py:319
  285.2 2.6 collective-permute-start.25
  285.2 6.8 %collective-permute-start.24 = (f32[8,512]{1,0:T(8,128)S(1)}, f32[8,512]{1,0:T(8,128)S(1)}, u32[]{:S(2)}, u32[]{:S(2)}) collective-permute-start(f32[8,512]{1,0:T(8,128)S(1)} %get-tuple-element.87.rest_1_), channel_id=1, source_target_pairs={{0,1},{1,2},{2,3},{3,4},{4,5},{5,6},{6,7},{7,8},{8,9},{9,10},{10,1... | collective-permute-start | bytes 49160 | tf_op jit(solution)/shard_map/ppermute | solution.py:319
  285.7 6.3 %collective-permute-start.27 = (f32[8,512]{1,0:T(8,128)S(1)}, f32[8,512]{1,0:T(8,128)S(1)}, u32[]{:S(2)}, u32[]{:S(2)}) collective-permute-start(f32[8,512]{1,0:T(8,128)S(1)} %get-tuple-element.88.rest_2_), channel_id=1, source_target_pairs={{0,28},{1,29},{2,30},{3,31},{4,0},{5,1},{6,2},{7,3},{8,4},{9,5},{1... | collective-permute-start | bytes 49160 | tf_op jit(solution)/shard_map/ppermute | solution.py:319
  285.7 6.5 %collective-permute-start.26 = (f32[8,512]{1,0:T(8,128)S(1)}, f32[8,512]{1,0:T(8,128)S(1)}, u32[]{:S(2)}, u32[]{:S(2)}) collective-permute-start(f32[8,512]{1,0:T(8,128)S(1)} %get-tuple-element.89.rest_3_), channel_id=1, source_target_pairs={{0,4},{1,5},{2,6},{3,7},{4,8},{5,9},{6,10},{7,11},{8,12},{9,13},{1... | collective-permute-start | bytes 49160 | tf_op jit(solution)/shard_map/ppermute | solution.py:319
  287.8 4.8 %collective-permute-start.29 = (f32[8,512]{1,0:T(8,128)S(1)}, f32[8,512]{1,0:T(8,128)S(1)}, u32[]{:S(2)}, u32[]{:S(2)}) collective-permute-start(f32[8,512]{1,0:T(8,128)S(1)} %get-tuple-element.90.rest_4_), channel_id=1, source_target_pairs={{0,16},{1,17},{2,18},{3,19},{4,20},{5,21},{6,22},{7,23},{8,24},{9,... | collective-permute-start | bytes 49160 | tf_op jit(solution)/shard_map/ppermute | solution.py:319
  287.8 5.1 %collective-permute-start.28 = (f32[8,512]{1,0:T(8,128)S(1)}, f32[8,512]{1,0:T(8,128)S(1)}, u32[]{:S(2)}, u32[]{:S(2)}) collective-permute-start(f32[8,512]{1,0:T(8,128)S(1)} %get-tuple-element.91.rest_5_), channel_id=1, source_target_pairs={{0,16},{1,17},{2,18},{3,19},{4,20},{5,21},{6,22},{7,23},{8,24},{9,... | collective-permute-start | bytes 49160 | tf_op jit(solution)/shard_map/ppermute | solution.py:319

commit v2 on v1

--- a/solution.py
+++ b/solution.py
@@ -250,8 +250,88 @@
     lax.fori_loop(0, m_tmp.shape[1] // LANES, body, 0)
 
 
+def greet(partners):
+    barrier = pltpu.get_barrier_semaphore()
+    for partner in partners:
+        pl.semaphore_signal(
+            barrier, inc=1, device_id=(partner,), device_id_type=pl.DeviceIdType.MESH
+        )
+    pl.semaphore_wait(barrier, len(partners))
+
+
+def face_copies(pieces, land_ref, send_sem, recv_sem, slots):
+    me = lax.axis_index("dev")
+    targets = [lax.rem(me + by + slots, slots) for by in FACE_STEPS]
+    greet(targets)
+    copies = [
+        pltpu.make_async_remote_copy(
+            src_ref=pieces[face],
+            dst_ref=land_ref.at[face ^ 1],
+            send_sem=send_sem.at[face],
+            recv_sem=recv_sem.at[face ^ 1],
+            device_id=(targets[face],),
+            device_id_type=pl.DeviceIdType.MESH,
+        )
+        for face in range(FACES)
+    ]
+    for copy in copies:
+        copy.start()
+    return copies
+
+
+def exchange_kernel(slots, *refs):
+    pieces, out_ref, (land_ref, send_sem, recv_sem) = refs[:FACES], refs[FACES], refs[FACES + 1 :]
+    cap = land_ref.shape[2]
+    for copy in face_copies(pieces, land_ref, send_sem, recv_sem, slots):
+        copy.wait()
+    for face in range(FACES):
+        out_ref[:, face * cap : (face + 1) * cap] = land_ref[face]
+
+
+def everyone_kernel(slots, total, own_ref, out_ref, land_ref, send_sem, recv_sem):
+    me = lax.axis_index("dev")
+    barrier = pltpu.get_barrier_semaphore()
+
+    def signal(by, carry):
+        pl.semaphore_signal(
+            barrier, inc=1, device_id=(lax.rem(me + by, slots),),
+            device_id_type=pl.DeviceIdType.MESH,
+        )
+        return carry
+
+    lax.fori_loop(1, slots, signal, 0)
+    pl.semaphore_wait(barrier, slots - 1)
+
+    def copy(by):
+        return pltpu.make_async_remote_copy(
+            src_ref=own_ref,
+            dst_ref=land_ref.at[me],
+            send_sem=send_sem.at[by],
+            recv_sem=recv_sem.at[by],
+            device_id=(lax.rem(me + by, slots),),
+            device_id_type=pl.DeviceIdType.MESH,
+        )
+
+    def start(by, carry):
+        copy(by).start()
+        return carry
+
+    def finish(by, carry):
+        copy(by).wait()
+        return carry
+
+    lax.fori_loop(1, slots, start, 0)
+    land_ref[me] = own_ref[...]
+    lax.fori_loop(1, slots, finish, 0)
+    if total:
+        out_ref[0] = jnp.sum(land_ref[...], axis=0)
+    else:
+        out_ref[...] = land_ref[...]
+
+
 def combine_kernel(cap, slots, initial, slot_ref, modes_ref, masks_ref, *rest):
-    own, far, rest = rest[:FACES], rest[FACES : 2 * FACES], rest[2 * FACES :]
+    own, rest = rest[:FACES], rest[FACES:]
+    rest, (far, send_sem, recv_sem) = rest[:-3], rest[-3:]
     if initial:
         rhs_ref, rhs_far_ref, out_ref, sums_ref = rest
     else:
@@ -259,10 +339,12 @@
     loads = own[0].shape[0]
     counts = MODES if initial else MODES + 4
     totals = [jnp.zeros((loads, cap), jnp.float32) for _ in range(counts)]
+    for copy in face_copies(own, far, send_sem, recv_sem, slots):
+        copy.wait()
     for face in range(FACES):
         span = slice(face * cap, (face + 1) * cap)
         shared = masks_ref[0:1, span]
-        value = own[face][...] - shared * far[face][...]
+        value = own[face][...] - shared * far[face]
         if initial:
             value = rhs_ref[:, span] - shared * rhs_far_ref[:, span] - value
         out_ref[:, span] = value
@@ -314,23 +396,43 @@
         compiler_params=params(),
     )(codes.reshape(1, nmax), jnp.stack([padded, dual_local[0]]))
 
-    def exchange(pieces):
+    def linked(name):
+        return pltpu.CompilerParams(
+            collective_id=name, has_side_effects=True, vmem_limit_bytes=50 * 2**20
+        )
+
+    def face_scratch(rows):
         return [
-            lax.ppermute(
-                pieces[face ^ 1], "dev",
-                [(i, (i - FACE_STEPS[face]) % slots) for i in range(slots)],
-            )
-            for face in range(FACES)
+            pltpu.VMEM((FACES, rows, cap), f32),
+            pltpu.SemaphoreType.DMA((FACES,)),
+            pltpu.SemaphoreType.DMA((FACES,)),
         ]
 
+    def everyone(block, total):
+        return pl.pallas_call(
+            functools.partial(everyone_kernel, slots, total),
+            out_shape=shape((1 if total else slots,) + block.shape, f32),
+            scratch_shapes=[
+                pltpu.VMEM((slots,) + block.shape, f32),
+                pltpu.SemaphoreType.DMA((slots,)),
+                pltpu.SemaphoreType.DMA((slots,)),
+            ],
+            compiler_params=linked(0 if total else 4),
+        )(block)
+
     both = jnp.concatenate([modes, rhs], axis=0)
-    far_pieces = exchange([both[:, f * cap : (f + 1) * cap] for f in range(FACES)])
+    far_both = pl.pallas_call(
+        functools.partial(exchange_kernel, slots),
+        out_shape=shape((2 * loads, nmax), f32),
+        scratch_shapes=face_scratch(2 * loads),
+        compiler_params=linked(3),
+    )(*[both[:, f * cap : (f + 1) * cap] for f in range(FACES)])
     position = jnp.arange(cap, dtype=jnp.int32)
     counted = position[None, :] < shared_counts[0][:, None]
     shared = (counted & (neighbours[0] >= 0)[:, None]).astype(f32).reshape(1, nmax)
     weights = counted.astype(f32).reshape(1, nmax) - 0.5 * shared
     masks = jnp.concatenate([shared, weights, jnp.zeros((6, nmax), f32)], axis=0)
-    far_both = jnp.concatenate(far_pieces, axis=1) * shared
+    far_both = far_both * shared
     far_modes, far_rhs = far_both[:loads], far_both[loads:]
 
     own6 = modes[:MODES].reshape(MODES, FACES, cap)
@@ -351,7 +453,8 @@
         else [row, jnp.pad(coarse_rhs[0], ((0, 0), (0, LANES - loads)))],
         axis=1,
     )
-    everything = lax.all_gather(row, "dev", axis=0, tiled=True)
+    everything = everyone(jnp.pad(row, ((0, loads - MODES), (0, 0))), False)
+    everything = everything[:, :MODES].reshape(size, row.shape[1])
     goal = jnp.pad(everything[:, size : size + loads].T, ((0, 0), (0, width - size)))
     matrix = jnp.pad(everything[:, :size], ((0, 0), (0, width - size)))
     inverted = pl.pallas_call(
@@ -387,16 +490,16 @@
     slot_array = my_slot.reshape(1).astype(jnp.int32)
 
     def combine(own, extra, initial):
-        far = exchange(own)
-        ins = (modes, masks, *own, *far, *extra)
+        ins = (modes, masks, *own, *extra)
         value, sums = pl.pallas_call(
             functools.partial(combine_kernel, cap, slots, initial),
             in_specs=[pl.BlockSpec(memory_space=pltpu.SMEM)]
             + [pl.BlockSpec(memory_space=pltpu.VMEM)] * len(ins),
             out_shape=(vector, sums_shape),
-            compiler_params=params(),
+            scratch_shapes=face_scratch(loads),
+            compiler_params=linked(1 if initial else 2),
         )(slot_array, *ins)
-        return value, lax.all_gather(sums, "dev", axis=0)
+        return value, everyone(sums, True)
 
     mult, *own = with_product(
         start_kernel, (goal, picks, modes, far_modes, code_table, inverse), (vector,)

time: 338 us -> 186 us (0.55)
  blocking collectives: 201 us -> 0 us
  Pallas kernels: 77.9 us -> 173 us
  starting transfers between devices: 34.3 us -> 0 us
  waiting for transfers between devices: 12.7 us -> 0 us
    all_gather x5 -> x0, blocking collectives: 201 us -> none  [the longest x4 162 us: combine(): return (value, lax.all_gather(sums, 'dev', axis=0))]
    pallas_call x0 -> x6, Pallas kernels: none -> 61.9 us  [the longest x5 51.4 us: everyone(): pl.pallas_call(functools.partial(everyone_kernel, slots, total), out_shap...]
    ppermute x30 -> x0, starting transfers between devices: 34.3 us -> none  [exchange(): lax.ppermute(pieces[face ^ 1], 'dev', [(i, (i - FACE_STEPS[face]) % slots...]
    pallas_call x4, Pallas kernels: 0.6 us -> 33.8 us  [combine(): pl.pallas_call(functools.partial(combine_kernel, cap, slots, initial), in...]
    ppermute x30 -> x0, waiting for transfers between devices: 12.7 us -> none  [exchange(): lax.ppermute(pieces[face ^ 1], 'dev', [(i, (i - FACE_STEPS[face]) % slots...]
  transfers between devices with their start and end apart: 30 -> 0, of which waited for: 18 -> 0; matrix products, arithmetic and copies ran while one was open for 1% -> 0% of each run, Pallas kernels for 0% -> 0%
where the time goes in v2:
time: 186 us
  Pallas kernels  173 us (93%)
  other arithmetic  5.5 us (3%)
  local copies, waits for them, and re-layouts  4.71 us (3%)
    pallas_call x4, Pallas kernels, with_product(): pl.pallas_call(functools.partial(kernel, steps, cap, *static), grid=(step...  53.2 us
    pallas_call x5, Pallas kernels, everyone(): pl.pallas_call(functools.partial(everyone_kernel, slots, total), out_shap...  51.4 us
    pallas_call x4, Pallas kernels, combine(): pl.pallas_call(functools.partial(combine_kernel, cap, slots, initial), in...  33.8 us
    pallas_call x1, Pallas kernels, per_device(): pl.pallas_call(invert_kernel, out_shape=shape((size, width), f32), compil...  16.5 us
    pallas_call x1, Pallas kernels, per_device(): pl.pallas_call(functools.partial(exchange_kernel, slots), out_shape=shape...  10.5 us
    pallas_call x1, Pallas kernels, per_device(): pl.pallas_call(functools.partial(last_kernel, cap, slots), out_shape=(sha...  4.04 us

profile of v2, /device:TPU:0, one launch (start us, length us, event | category | flops | bytes accessed | tf_op | source)
XLA Modules:
  0.0 185.6 jit_solution(13408845716395316040)
XLA Ops:
  1.5 0.7 compare_bitcast_fusion
  2.2 0.1 pad.34.clone
  2.3 0.1 broadcast_in_dim.189
  2.5 0.1 broadcast_in_dim.225
  2.7 0.1 broadcast_in_dim.219
  2.9 0.1 broadcast_in_dim.213
  3.1 0.1 broadcast_in_dim.207
  3.3 0.1 broadcast_in_dim.201
  3.5 0.1 broadcast_in_dim.195
  3.6 0.7 copy.43
  4.3 0.7 fusion.2.map_ref
  5.0 0.7 compare_select_fusion.codes_ref
  5.7 0.7 subtract_bitcast_fusion
  6.5 0.7 fusion.1
  7.3 0.9 copy.42
  8.2 0.9 pad_maximum_fusion.values_ref
  9.1 3.5 %shard_map.95 = (f32[8,3072]{1,0:T(8,128)S(1)}, f32[8,3072]{1,0:T(8,128)S(1)}, s32[24,128]{1,0:T(8,128)S(1)}) custom-call(s32[1,3072]{1,0:T(1,128)S(1)} %compare_select_fusion.codes_ref, f32[2,8,3072]{2,1,0:T(8,128)S(1)} %pad_maximum_fusion.values_ref), custom_call_target="tpu_custom_call" | custom-call | tf_op jit(solution)/shard_map/pallas_call | solution.py:389
  12.6 0.3 fusion.4
  12.9 0.1 broadcast_in_dim.192
  13.1 10.5 %shard_map.96 = f32[16,3072]{1,0:T(8,128)S(1)} custom-call(f32[16,512]{1,0:T(8,128)S(1)} %get-tuple-element.114.refs_0_, f32[16,512]{1,0:T(8,128)S(1)} %get-tuple-element.113.refs_1_, f32[16,512]{1,0:T(8,128)S(1)} %get-tuple-element.112.refs_2_, f32[16,512]{1,0:T(8,128)S(1)} %get-tuple-element.111.refs_3_, f32[16,512]{1,0:T(8,128)S(1)} %get-tuple-element.110.refs_4_, ...), custom_call_target="tpu_custom_call" | custom-call | tf_op jit(solution)/shard_map/pallas_call | solution.py:424
  23.6 0.3 convolution_negate_fusion
  23.9 0.1 fusion.6
  24.0 0.1 broadcast_in_dim.199
  24.2 0.1 broadcast_in_dim.229
  24.3 0.1 broadcast_in_dim.223
  24.4 0.1 broadcast_in_dim.217
  24.5 0.1 broadcast_in_dim.211
  24.7 0.1 broadcast_in_dim.205
  24.9 9.2 %shard_map.97 = f32[32,8,256]{2,1,0:T(8,128)S(1)} custom-call(f32[8,256]{1,0:T(8,128)S(1)} %pad.26.own_ref), custom_call_target="tpu_custom_call" | custom-call | tf_op jit(solution)/shard_map/pallas_call | solution.py:412
  34.1 0.1 slice.90
  34.3 0.7 broadcast_select_fusion.matrix_ref
  34.9 16.5 %shard_map.98 = f32[192,256]{1,0:T(8,128)S(1)} custom-call(f32[192,256]{1,0:T(8,128)S(1)} %broadcast_select_fusion.matrix_ref), custom_call_target="tpu_custom_call" | custom-call | tf_op jit(solution)/shard_map/pallas_call | solution.py:460
  51.5 0.4 concatenate.15
  51.9 0.1 copy.34
  52.0 0.1 select_bitcast_fusion.picks_ref
  52.1 13.3 %shard_map.99 = (f32[8,3072]{1,0:T(8,128)S(1)}, f32[8,512]{1,0:T(8,128)S(1)}, f32[8,512]{1,0:T(8,128)S(1)}, f32[8,512]{1,0:T(8,128)S(1)}, f32[8,512]{1,0:T(8,128...) custom-call(f32[8,256]{1,0:T(8,128)S(1)} %pad.27.coarse_ref, f32[256,128]{1,0:T(8,128)S(1)} %select_bitcast_fusion.picks_ref, ...), custom_call_target="tpu_custom_call" | custom-call | tf_op jit(solution)/shard_map/pallas_call | solution.py:479
  65.4 9.1 %shard_map.100 = (f32[8,3072]{1,0:T(8,128)S(1)}, f32[8,256]{1,0:T(8,128)S(1)}) custom-call(s32[1]{0:T(128)} %bitcast.slot_ref, f32[8,3072]{1,0:T(8,128)S(1)} %get-tuple-element.51.modes_ref, f32[8,3072]{1,0:T(8,128)S(1)} %get-tuple-element.123.masks_ref, f32[8,512]{1,0:T(8,128)S(1)} %get-tuple-element.54.rest_0_, f32[8,512]{1,0:T(8,128)S(1)} %get-tuple-element.55.rest_1_, ...), custom_call_target="tpu_custom_call" | custom-call | tf_op jit(solution)/shard_map/pallas_call | solution.py:494
  74.5 10.5 %shard_map.101.gathered_ref = f32[1,8,256]{2,1,0:T(8,128)S(1)} custom-call(f32[8,256]{1,0:T(8,128)S(1)} %get-tuple-element.60.own_ref), custom_call_target="tpu_custom_call" | custom-call | tf_op jit(solution)/shard_map/pallas_call | solution.py:412
  85.0 13.3 %shard_map.102 = (f32[8,3072]{1,0:T(8,128)S(1)}, f32[8,512]{1,0:T(8,128)S(1)}, f32[8,512]{1,0:T(8,128)S(1)}, f32[8,512]{1,0:T(8,128)S(1)}, f32[8,512]{1,0:T(8,12...) custom-call(f32[1,8,256]{2,1,0:T(8,128)S(1)} %shard_map.101.gathered_ref, ...), custom_call_target="tpu_custom_call" | custom-call | tf_op jit(solution)/shard_map/pallas_call | solution.py:479
  98.3 8.2 %shard_map.103 = (f32[8,3072]{1,0:T(8,128)S(1)}, f32[8,256]{1,0:T(8,128)S(1)}) custom-call(s32[1]{0:T(128)} %bitcast.slot_ref, f32[8,3072]{1,0:T(8,128)S(1)} %get-tuple-element.51.modes_ref, f32[8,3072]{1,0:T(8,128)S(1)} %get-tuple-element.123.masks_ref, f32[8,512]{1,0:T(8,128)S(1)} %get-tuple-element.62.rest_0_, f32[8,512]{1,0:T(8,128)S(1)} %get-tuple-element.63.rest_1_, ...), custom_call_target="tpu_custom_call" | custom-call | tf_op jit(solution)/shard_map/pallas_call | solution.py:494
  106.6 10.6 %shard_map.104.gathered_ref = f32[1,8,256]{2,1,0:T(8,128)S(1)} custom-call(f32[8,256]{1,0:T(8,128)S(1)} %get-tuple-element.69.own_ref), custom_call_target="tpu_custom_call" | custom-call | tf_op jit(solution)/shard_map/pallas_call | solution.py:412
  117.2 13.3 %shard_map.105 = (f32[8,3072]{1,0:T(8,128)S(1)}, f32[8,3072]{1,0:T(8,128)S(1)}, f32[8,3072]{1,0:T(8,128)S(1)}, f32[8,3072]{1,0:T(8,128)S(1)}, f32[8,3072]{1,0:T(...) custom-call(f32[1,8,256]{2,1,0:T(8,128)S(1)} %shard_map.104.gathered, ...), custom_call_target="tpu_custom_call" | custom-call | tf_op jit(solution)/shard_map/pallas_call | solution.py:479
  130.5 8.2 %shard_map.106 = (f32[8,3072]{1,0:T(8,128)S(1)}, f32[8,256]{1,0:T(8,128)S(1)}) custom-call(s32[1]{0:T(128)} %bitcast.slot_ref, f32[8,3072]{1,0:T(8,128)S(1)} %get-tuple-element.51.modes_ref, f32[8,3072]{1,0:T(8,128)S(1)} %get-tuple-element.123.masks_ref, f32[8,512]{1,0:T(8,128)S(1)} %get-tuple-element.72.rest_0_, f32[8,512]{1,0:T(8,128)S(1)} %get-tuple-element.73.rest_1_, ...), custom_call_target="tpu_custom_call" | custom-call | tf_op jit(solution)/shard_map/pallas_call | solution.py:494
  138.8 10.6 %shard_map.107.gathered_ref = f32[1,8,256]{2,1,0:T(8,128)S(1)} custom-call(f32[8,256]{1,0:T(8,128)S(1)} %get-tuple-element.81.own_ref), custom_call_target="tpu_custom_call" | custom-call | tf_op jit(solution)/shard_map/pallas_call | solution.py:412
  149.4 13.3 %shard_map.108 = (f32[8,3072]{1,0:T(8,128)S(1)}, f32[8,3072]{1,0:T(8,128)S(1)}, f32[8,3072]{1,0:T(8,128)S(1)}, f32[8,3072]{1,0:T(8,128)S(1)}, f32[8,3072]{1,0:T(...) custom-call(f32[1,8,256]{2,1,0:T(8,128)S(1)} %shard_map.107.gathered, ...), custom_call_target="tpu_custom_call" | custom-call | tf_op jit(solution)/shard_map/pallas_call | solution.py:479
  162.7 8.2 %shard_map.109 = (f32[8,3072]{1,0:T(8,128)S(1)}, f32[8,256]{1,0:T(8,128)S(1)}) custom-call(s32[1]{0:T(128)} %bitcast.slot_ref, f32[8,3072]{1,0:T(8,128)S(1)} %get-tuple-element.51.modes_ref, f32[8,3072]{1,0:T(8,128)S(1)} %get-tuple-element.123.masks_ref, f32[8,512]{1,0:T(8,128)S(1)} %get-tuple-element.86.rest_0_, f32[8,512]{1,0:T(8,128)S(1)} %get-tuple-element.87.rest_1_, ...), custom_call_target="tpu_custom_call" | custom-call | tf_op jit(solution)/shard_map/pallas_call | solution.py:494
  170.9 10.6 %shard_map.110.gathered_ref = f32[1,8,256]{2,1,0:T(8,128)S(1)} custom-call(f32[8,256]{1,0:T(8,128)S(1)} %get-tuple-element.95.own_ref), custom_call_target="tpu_custom_call" | custom-call | tf_op jit(solution)/shard_map/pallas_call | solution.py:412
  181.5 4.0 %shard_map.111 = (f32[1,8,3072]{2,1,0:T(8,128)}, f32[1,8,3072]{2,1,0:T(8,128)}) custom-call(f32[1,8,256]{2,1,0:T(8,128)S(1)} %shard_map.110.gathered_ref, f32[256,128]{1,0:T(8,128)S(1)} %select_bitcast_fusion.picks_ref, f32[8,3072]{1,0:T(8,128)S(1)} %get-tuple-element.51.modes_ref, f32[8,3072]{1,0:T(8,128)S(1)} %get-tuple-element.101.far_ref, ...), custom_call_target="tpu_custom_call" | custom-call | tf_op jit(solution)/shard_map/pallas_call | solution.py:522
  (43 shorter events, 1.0 us)
